TPU v7x, 128 devices: a whole 4x4x4 slice. The times are simulated.
128 devices in a mesh: row: 32 (over z, y, core), col: 4 (over x).
Axes of the slice: x: 4, y: 4, z: 4, core: 2. Of those that a mesh axis runs over, the one named last changes fastest.
Arguments:
- matrix: float32 [1, 32, 512, 8, 4, 512], P(None, 'row', None, None, 'col'), may hold values from -30 to 30, as said below
Outputs:
- factored: float32 [1, 32, 512, 8, 4, 512], P(None, 'row', None, None, 'col')
Inputs may be any that keep to these rules, and one draw needn't show every extreme that they name: matrix is symmetric, positive definite and well conditioned.
All inputs are finite; a program needn't handle non-finite values.
Results may differ from a plain program's by a relative error of at most 0.00013.
Values sent between devices are 32-bit elements; how exact they have to be, the bound alone decides.
A program may use at most 192 MiB of HBM per device.

v0:
```python
import jax
import jax.numpy as jnp
from jax import lax
from jax.sharding import PartitionSpec as P

NB = 512
STEPS = 2


def spread(value, axis, source):
    kept = jnp.where(lax.axis_index(axis) == source, value, 0).astype(value.dtype)
    return lax.psum(kept, axis)


def from_root(shard, axis, root):
    return lax.dynamic_index_in_dim(lax.all_gather(shard, axis), root, 0, keepdims=False)


def trailing_product(column_panel, transposed):
    return jnp.einsum(
        "tan,sbn->tasb",
        column_panel,
        transposed,
        precision=lax.Precision.HIGHEST,
        preferred_element_type=jnp.float32,
    )


def shards(matrix):
    local_rows = matrix.shape[0]
    local_cols = matrix.shape[3]
    blocks = matrix.reshape(local_rows, NB, local_cols, NB)
    row_count = lax.axis_size("row")
    column_count = lax.axis_size("col")
    group_size = row_count // column_count
    row_place = lax.axis_index("row")
    column_place = lax.axis_index("col")
    tile_rows = jnp.arange(local_rows, dtype=jnp.int32) * row_count + row_place
    tile_columns = jnp.arange(local_cols, dtype=jnp.int32) * column_count + column_place
    anchor = jnp.int32(0)

    def fetch_columns(column_panel):
        empty = jnp.zeros((local_rows, group_size, NB, NB), jnp.float32)
        slot_index = row_place // column_count
        holder = row_place % column_count == column_place
        contribution = jnp.where(holder, column_panel, 0.0)
        filled = lax.dynamic_update_slice(
            empty, contribution[:, None], (anchor, slot_index, anchor, anchor)
        )
        gathered = lax.psum(filled, "row")
        return gathered.reshape(local_cols, NB, NB)

    def factor_step(blocks, step):
        root_row = step % row_count
        local_row = step // row_count
        root_col = step % column_count
        local_col = step // column_count
        corner = blocks[local_row, :, local_col, :]
        owner = (row_place == root_row) & (column_place == root_col)
        identity = jnp.eye(NB, dtype=jnp.float32)
        chosen = jnp.where(owner, corner, identity)
        factor_local = jnp.linalg.cholesky(chosen)
        diag_block = spread(factor_local, "row", root_row)
        source = blocks[:, :, local_col, :]
        solved = jax.scipy.linalg.solve_triangular(
            diag_block, source.reshape(local_rows * NB, NB).T, lower=True
        ).T
        solved = solved.reshape(local_rows, NB, NB)
        panel_local = jnp.where((tile_rows > step)[:, None, None], solved, 0.0)
        column_panel = from_root(panel_local, "col", root_col)
        transposed = fetch_columns(column_panel)
        return (diag_block, column_panel, transposed)

    factors = factor_step(blocks, 0)
    for step in range(STEPS):
        diag_block, column_panel, transposed = factors
        write_blocks = blocks
        write_local_row = step // row_count
        write_local_col = step // column_count
        column_now = write_blocks[:, :, write_local_col, :]
        owns_col = column_place == step % column_count
        row_after = (tile_rows > step)[:, None, None]
        row_hit = (tile_rows == step)[:, None, None]
        new_column = jnp.where(
            row_after, column_panel, jnp.where(row_hit, diag_block[None], column_now)
        )
        new_column = jnp.where(owns_col, new_column, column_now)
        write_blocks = write_blocks.at[:, :, write_local_col, :].set(new_column)
        row_now = write_blocks[write_local_row]
        owns_row = row_place == step % row_count
        zero_cols = (tile_columns > step)[None, :, None]
        new_row = jnp.where(owns_row & zero_cols, 0.0, row_now)
        blocks = write_blocks.at[write_local_row].set(new_row)
        if step + 1 < STEPS:
            next_col = (step + 1) // column_count
            single = trailing_product(column_panel, transposed[next_col : next_col + 1])
            blocks = blocks.at[:, :, next_col, :].set(
                blocks[:, :, next_col, :] - single[:, :, 0, :]
            )
            factors = factor_step(blocks, step + 1)
            rest = transposed.at[next_col].set(jnp.zeros((NB, NB), jnp.float32))
            blocks = blocks - trailing_product(column_panel, rest)
        else:
            blocks = blocks - trailing_product(column_panel, transposed)
    return blocks.reshape(matrix.shape)


def solution(mesh):
    in_specs = (P(None, "row", None, None, "col", None),)
    out_specs = P(None, "row", None, None, "col", None)
    return jax.shard_map(shards, mesh=mesh, in_specs=in_specs, out_specs=out_specs, check_vma=False)
```

profile of v0, /device:TPU:47, one launch (start us, length us, event | category | flops | bytes accessed | tf_op | source)
XLA Modules:
  0.0 933.7 jit_solution(8377719153286255205)
XLA Ops:
  6.5 20.5 %copy.2 = f32[1,1,512,8,1,512]{2,5,3,4,1,0:T(8,128)} copy(f32[1,1,512,8,1,512]{5,4,3,2,1,0:T(1,128)} %param.16) | data formatting | bytes 16777216 | tf_op args[0]
  30.2 11.7 %cholesky.286 = f32[128,128]{1,0:T(8,128)S(1)} custom-call(f32[128,128]{1,0:T(8,128)S(1)} %cholesky.426), custom_call_target="Cholesky" | custom-call | tf_op jit(solution)/shard_map/jit(cholesky)/cholesky | solution.py:62
  42.1 9.8 %custom-call.27 = f32[1,128,128]{1,2,0:T(8,128)S(1)} custom-call(f32[1,128,128]{2,1,0:T(8,128)S(1)} %get-tuple-element.136), custom_call_target="InvertDiagBlocksLowerTriangular" | custom-call | tf_op jit(solution)/shard_map/jit(cholesky)/cholesky | solution.py:62
  52.7 11.7 %cholesky.305 = f32[128,128]{1,0:T(8,128)S(1)} custom-call(f32[128,128]{1,0:T(8,128)S(1)} %cholesky.430), custom_call_target="Cholesky" | custom-call | tf_op jit(solution)/shard_map/jit(cholesky)/cholesky | solution.py:62
  64.6 9.9 %custom-call.28 = f32[1,128,128]{1,2,0:T(8,128)S(1)} custom-call(f32[1,128,128]{2,1,0:T(8,128)S(1)} %get-tuple-element.134), custom_call_target="InvertDiagBlocksLowerTriangular" | custom-call | tf_op jit(solution)/shard_map/jit(cholesky)/cholesky | solution.py:62
  75.6 11.7 %cholesky.326 = f32[128,128]{1,0:T(8,128)S(1)} custom-call(f32[128,128]{1,0:T(8,128)S(1)} %cholesky.435), custom_call_target="Cholesky" | custom-call | tf_op jit(solution)/shard_map/jit(cholesky)/cholesky | solution.py:62
  87.5 9.8 %custom-call.29 = f32[1,128,128]{1,2,0:T(8,128)S(1)} custom-call(f32[1,128,128]{2,1,0:T(8,128)S(1)} %get-tuple-element.132), custom_call_target="InvertDiagBlocksLowerTriangular" | custom-call | tf_op jit(solution)/shard_map/jit(cholesky)/cholesky | solution.py:62
  98.1 11.9 %cholesky.343 = f32[128,128]{1,0:T(8,128)S(1)} custom-call(f32[128,128]{1,0:T(8,128)S(1)} %convolution_subtract_fusion.12), custom_call_target="Cholesky" | custom-call | tf_op jit(solution)/shard_map/jit(cholesky)/cholesky | solution.py:62
  117.4 104.2 %all-reduce.6.cloned.1.call-done = f32[512,512]{0,1:T(8,128)} async-done(((f32[512,512]{0,1:T(8,128)}), f32[512,512]{0,1:T(8,128)}) %all-reduce.6.cloned.1.call-update) | async-done | bytes 1048592 | tf_op jit(solution)/shard_map/psum | solution.py:12
  222.9 8.2 while.10
  231.9 40.1 %custom-call.30 = f32[4,128,128]{1,2,0:T(8,128)S(1)} custom-call(f32[4,128,128]{2,1,0:T(8,128)} %copy-done.4), custom_call_target="InvertDiagBlocksLowerTriangular" | custom-call | tf_op jit(solution)/shard_map/jit(_solve_triangular)/triangular_solve | solution.py:65
  276.6 48.0 %all-gather.5.cloned.1.call-done = f32[2048,512]{0,1:T(8,128)} async-done(((f32[512,512]{0,1:T(8,128)}), f32[2048,512]{0,1:T(8,128)}) %all-gather.5.cloned.1.call-update) | async-done | bytes 4194320 | tf_op jit(solution)/shard_map/all_gather | solution.py:16
  326.2 4.3 broadcast.342
  334.7 8.5 broadcast_select_fusion
  343.1 109.7 %all-reduce.8.cloned.1.call-done = f32[1,8,512,512]{3,2,1,0:T(8,128)} async-done(((f32[1,8,512,512]{3,2,1,0:T(8,128)}), f32[1,8,512,512]{3,2,1,0:T(8,128)}) %all-reduce.8.cloned.1.call-update) | async-done | bytes 8388624 | tf_op jit(solution)/shard_map/psum | solution.py:50
  452.8 3.7 convert_select_fusion
  458.2 11.7 %cholesky.358 = f32[128,128]{1,0:T(8,128)S(1)} custom-call(f32[128,128]{1,0:T(8,128)S(1)} %cholesky.439), custom_call_target="Cholesky" | custom-call | tf_op jit(solution)/shard_map/jit(cholesky)/cholesky | solution.py:62
  470.1 9.8 %custom-call.31 = f32[1,128,128]{1,2,0:T(8,128)S(1)} custom-call(f32[1,128,128]{2,1,0:T(8,128)S(1)} %get-tuple-element.130), custom_call_target="InvertDiagBlocksLowerTriangular" | custom-call | tf_op jit(solution)/shard_map/jit(cholesky)/cholesky | solution.py:62
  482.5 11.9 %cholesky.377 = f32[128,128]{1,0:T(8,128)S(1)} custom-call(f32[128,128]{1,0:T(8,128)S(1)} %cholesky.443), custom_call_target="Cholesky" | custom-call | tf_op jit(solution)/shard_map/jit(cholesky)/cholesky | solution.py:62
  494.5 9.8 %custom-call.32 = f32[1,128,128]{1,2,0:T(8,128)S(1)} custom-call(f32[1,128,128]{2,1,0:T(8,128)S(1)} %get-tuple-element.128), custom_call_target="InvertDiagBlocksLowerTriangular" | custom-call | tf_op jit(solution)/shard_map/jit(cholesky)/cholesky | solution.py:62
  506.4 11.7 %cholesky.398 = f32[128,128]{1,0:T(8,128)S(1)} custom-call(f32[128,128]{1,0:T(8,128)S(1)} %cholesky.448), custom_call_target="Cholesky" | custom-call | tf_op jit(solution)/shard_map/jit(cholesky)/cholesky | solution.py:62
  518.2 9.8 %custom-call.33 = f32[1,128,128]{1,2,0:T(8,128)S(1)} custom-call(f32[1,128,128]{2,1,0:T(8,128)S(1)} %get-tuple-element.126), custom_call_target="InvertDiagBlocksLowerTriangular" | custom-call | tf_op jit(solution)/shard_map/jit(cholesky)/cholesky | solution.py:62
  529.9 11.7 %cholesky.415 = f32[128,128]{1,0:T(8,128)S(1)} custom-call(f32[128,128]{1,0:T(8,128)S(1)} %convolution_subtract_fusion.11), custom_call_target="Cholesky" | custom-call | tf_op jit(solution)/shard_map/jit(cholesky)/cholesky | solution.py:62
  548.3 104.6 %all-reduce.10.cloned.1.call-done = f32[512,512]{0,1:T(8,128)} async-done(((f32[512,512]{0,1:T(8,128)}), f32[512,512]{0,1:T(8,128)}) %all-reduce.10.cloned.1.call-update) | async-done | bytes 1048592 | tf_op jit(solution)/shard_map/psum | solution.py:12
  654.3 8.7 while.11
  663.0 39.3 %custom-call.34 = f32[4,128,128]{1,2,0:T(8,128)S(1)} custom-call(f32[4,128,128]{2,1,0:T(8,128)S(1)} %get-tuple-element.94), custom_call_target="InvertDiagBlocksLowerTriangular" | custom-call | tf_op jit(solution)/shard_map/jit(_solve_triangular)/triangular_solve | solution.py:65
  708.5 47.8 %all-gather.7.cloned.1.call-done = f32[2048,512]{1,0:T(8,128)} async-done(((f32[512,512]{1,0:T(8,128)}), f32[2048,512]{1,0:T(8,128)}) %all-gather.7.cloned.1.call-update) | async-done | bytes 4194320 | tf_op jit(solution)/shard_map/all_gather | solution.py:16
  760.6 4.3 broadcast.351
  768.2 16.7 %bitcast_subtract_fusion = f32[1,512,8,512]{1,3,2,0:T(8,128)S(1)} fusion(f32[1,512,8,512]{1,3,2,0:T(8,128)} %bitcast_dynamic-update-slice_fusion.3, f32[8,512,512]{2,1,0:T(8,128)} %broadcast_dynamic-update-slice_fusion, f32[2048,512]{0,1:T(8,128)} %all-gather.5.cloned.1.call-done), kind=kOutput, calls=%fused_computation.4 | convolution fusion | flops 12886999040 | bytes 26214400 | tf_op jit(solution)/shard_map/tan,sbn->tasb/dot_general | solution.py:20
  789.6 97.6 %all-reduce.12.cloned.1.call-done = f32[8,512,512]{2,1,0:T(8,128)} async-done(((f32[8,512,512]{2,1,0:T(8,128)}), f32[8,512,512]{2,1,0:T(8,128)}) %all-reduce.12.cloned.1.call-update) | async-done | bytes 8388624 | tf_op jit(solution)/shard_map/psum | solution.py:50
  887.2 18.7 %subtract_bitcast_fusion = f32[1,1,512,8,1,512]{2,5,3,4,1,0:T(8,128)} fusion(f32[512,8,512]{0,2,1:T(8,128)} %bitcast_dynamic-update-slice_fusion.2, pred[8]{0:T(512)(128)(4,1)S(1)} %compare_and_fusion.1, f32[8,512,512]{2,1,0:T(8,128)} %all-reduce.12.cloned.1.call-done, f32[2048,512]{1,0:T(8,128)} %all-gather.7.cloned.1.call-done), kind=kOutput, calls=%fused_computation.5 | convolution fusion | flops 12889096192 | bytes 26214408 | tf_op jit(solution)/shard_map/tan,sbn->tasb/dot_general | solution.py:20
  905.9 20.5 %copy.35 = f32[1,1,512,8,1,512]{5,4,3,2,1,0:T(1,128)} copy(f32[1,1,512,8,1,512]{2,5,3,4,1,0:T(8,128)} %subtract_bitcast_fusion) | data formatting | bytes 16777216 | tf_op jit(solution)/shard_map/reshape | solution.py:105
  (163 shorter events, 72.1 us)
Async XLA Ops:
  6.5 215.0 %all-reduce.6.cloned.1.call-start = ((), (), s32[]{:S(2)}) async-start(), calls=%async_computation | async-start | bytes 2097152 | tf_op jit(solution)/shard_map/psum | solution.py:12
  115.9 208.7 %all-gather.5.cloned.1.call-start = ((), (), s32[]{:S(2)}) async-start(), calls=%async_computation.4 | async-start | bytes 5242880 | tf_op jit(solution)/shard_map/all_gather | solution.py:16
  231.2 0.7 copy-start.4
  276.5 176.4 %all-reduce.8.cloned.1.call-start = ((), (), s32[]{:S(2)}) async-start(), calls=%async_computation.1 | async-start | bytes 16777216 | tf_op jit(solution)/shard_map/psum | solution.py:50
  326.2 5.8 copy-start
  331.6 321.3 %all-reduce.10.cloned.1.call-start = ((), (), s32[]{:S(2)}) async-start(), calls=%async_computation.2 | async-start | bytes 2097152 | tf_op jit(solution)/shard_map/psum | solution.py:12
  457.1 1.1 copy-start.2
  548.3 208.0 %all-gather.7.cloned.1.call-start = ((), (), s32[]{:S(2)}) async-start(), calls=%async_computation.5 | async-start | bytes 5242880 | tf_op jit(solution)/shard_map/all_gather | solution.py:16
  702.3 1.8 copy-start.3
  708.2 179.1 %all-reduce.12.cloned.1.call-start = ((), (), s32[]{:S(2)}) async-start(), calls=%async_computation.3 | async-start | bytes 16777216 | tf_op jit(solution)/shard_map/psum | solution.py:50
  784.9 3.4 copy-start.1
Sparse Core Ops, SparseCore 0:
  116.0 105.5 all-reduce.5
  276.6 47.9 all-gather.4
  331.7 121.0 all-reduce.7
  548.4 104.4 all-reduce.9
  708.3 47.9 all-gather.6
  766.1 121.0 all-reduce.11
where the time goes:
time: 947 us; the launch traced here: 934 us
  waiting for transfers between devices  512 us (54%)
  other arithmetic  263 us (28%)
  local copies, waits for them, and re-layouts  83.1 us (9%)
  matrix products  55.1 us (6%)
  between operations  19.8 us (2%)
    psum x2, waiting for transfers between devices, spread(): return lax.psum(kept, axis)  209 us
    psum x2, waiting for transfers between devices, fetch_columns(): gathered = lax.psum(filled, 'row')  207 us
    another operation x29, other arithmetic, factor_step(): factor_local = jnp.linalg.cholesky(chosen)  158 us
    all_gather x2, waiting for transfers between devices, from_root(): lax.all_gather(shard, axis)  95.8 us
    another operation x5, other arithmetic, factor_step(): jax.scipy.linalg.solve_triangular(diag_block, source.reshape(local_rows *...  82.1 us
    dot_general x3, matrix products, trailing_product(): jnp.einsum('tan,sbn->tasb', column_panel, transposed, precision=lax.Preci...  39.1 us
    unnamed x13, local copies, waits for them, and re-layouts  26 us
    reshape x1, local copies, waits for them, and re-layouts, shards(): return blocks.reshape(matrix.shape)  20.5 us
  transfers between devices with their start and end apart: 6, of which 6 were waited for; matrix products, arithmetic and copies ran while one was open for 4% of the time, Pallas kernels for 0%

commit v1 on v0

v1 whole, which is shorter than its diff:
```python
import functools
import jax
import jax.numpy as jnp
from jax import lax
from jax.experimental import pallas as pl
from jax.experimental.pallas import tpu as pltpu
from jax.sharding import PartitionSpec as P

F32 = jnp.float32
BF = jnp.bfloat16
MESH = pl.DeviceIdType.MESH
NT = (((1,), (1,)), ((), ()))
NN = (((1,), (0,)), ((), ()))
NB = 512
Q = 128


def split(x):
    h=x.astype(BF)
    return h,(x-h.astype(F32)).astype(BF)

def dot3(a,b,dims):
    ah,al=a; bh,bl=b
    d=functools.partial(lax.dot_general,dimension_numbers=dims,preferred_element_type=F32)
    return d(ah,bh)+d(ah,bl)+d(al,bh)

def factor128(D):
    D3=[D[8*i:8*i+8,:] for i in range(16)]
    lane=lax.broadcasted_iota(jnp.int32,(8,128),1)
    sub=lax.broadcasted_iota(jnp.int32,(8,128),0)
    E3=[jnp.where(lane==sub+8*i,1.0,0.0).astype(F32) for i in range(16)]
    def bs(x,k): return jnp.broadcast_to(x[k:k+1,:],(8,128))
    U=[None]*16
    for b in range(16):
        c=8*b
        B={}
        for i in range(b,16):
            for k in range(8):
                B[i,k]=jnp.broadcast_to(D3[i][:,c+k:c+k+1],(8,128))
        g={(k,m):bs(B[b,m],k) for m in range(8) for k in range(m,8)}
        r=[None]*8; s={}
        for m in range(8):
            r[m]=lax.rsqrt(g[m,m])
            for k in range(m+1,8): s[k,m]=g[k,m]*r[m]
            for l in range(m+1,8):
                for k in range(l,8):
                    g[k,l]=g[k,l]-s[k,m]*s[l,m]
        T=D3[b]; Te=E3[b]
        urow=[];erow=[]
        for i in range(b,16):
            mk=[]
            for k in range(8):
                v=B[i,k]
                for m in range(k): v=v-mk[m]*s[k,m]
                mk.append(v*r[k])
            if i==b:
                oU=jnp.zeros((8,128),F32); oE=oU
                for k in range(8):
                    u=bs(T,k)*r[k]; e=bs(Te,k)*r[k]
                    urow.append(u); erow.append(e)
                    oU=jnp.where(sub==k,u,oU); oE=jnp.where(sub==k,e,oE)
                    if k<7:
                        mm=jnp.where(sub>k,mk[k],0.0)
                        T=T-mm*u; Te=Te-mm*e
                U[b]=jnp.where(lane>=sub+c,oU,0.0); E3[b]=oE
            else:
                d=D3[i]; e=E3[i]
                for k in range(8):
                    d=d-mk[k]*urow[k]; e=e-mk[k]*erow[k]
                D3[i]=d; E3[i]=e
    return jnp.concatenate(U,0), jnp.concatenate(E3,0)

def factor_tile(M):
    row=lax.broadcasted_iota(jnp.int32,(1024,128),0)
    def body(k,_):
        c0=pl.multiple_of(k*128,128)
        U,Linv=factor128(M[pl.ds(c0,128),pl.ds(c0,128)])
        P=M[:,pl.ds(c0,128)]
        X=dot3(split(P),split(Linv),NT)
        X=jnp.where(jnp.logical_or(row>=c0+128,row>=512),X,0.0)
        M[:,pl.ds(c0,128)]=X
        M[pl.ds(c0,128),pl.ds(c0,128)]=U.T
        Xl=jnp.where(row[:512]>=c0+128,X[:512],0.0)
        lh,ll=split(Xl)
        for rr in range(4):
            xh,xl=split(X[rr*256:(rr+1)*256])
            M[rr*256:(rr+1)*256,:]-=dot3((xh,xl),(lh,ll),NT)
        return 0
    lax.fori_loop(0,4,body,0)

LEADS = 3
ITEMS = [("L", 0), ("L", 1), ("L", 2)] + [("U", k, s) for s in range(8) for k in range(2)]
NITEM = len(ITEMS)


def place():
    row = lax.axis_index("row")
    return lax.rem(row, 2), lax.rem(row // 2, 4), row // 8, lax.axis_index("col")


def device(y, z, core, x):
    return ((lax.rem(z + 4, 4) * 4 + lax.rem(y + 4, 4)) * 2 + core, lax.rem(x + 4, 4))


def to_tree(t, y, z):
    if t == 0:
        return y, z
    if t == 1:
        return lax.rem(4 - y, 4), lax.rem(4 - z, 4)
    if t == 2:
        return z, y
    return lax.rem(4 - z, 4), lax.rem(4 - y, 4)


def children(t, y, z):
    u, v = to_tree(t, y, z)
    steps = {0: ((1, 0), (0, 1)), 1: ((-1, 0), (0, -1)), 2: ((0, 1), (1, 0)), 3: ((0, -1), (-1, 0))}
    (uy, uz), (vy, vz) = steps[t]
    return (
        ((v == 0) & (u < 3), uy, uz),
        ((u >= 1) & (v < 3), vy, vz),
        ((u == 1) & (v >= 1), -uy, -uz),
    )


def comm_kernel(mat, out, ap_out, buf, ap, load_sem, x_send, x_recv, x_last, t_send, t_recv, p_send, out_sem):
    core, y, z, x = place()
    root = (y == 0) & (z == 0)
    other = 1 - core

    def tile_load(s, dst, sem):
        return [
            pltpu.make_async_copy(mat.at[:, 4 * s + b, 0, :], dst.at[:, pl.ds(128 * b, 128)], sem.at[b])
            for b in range(4)
        ]

    for k in range(2):
        @pl.when(x == k)
        def _():
            for c in tile_load(0, ap.at[k], load_sem.at[8]):
                c.start()

    def item_rows(n):
        return pl.ds(n * NB, NB)

    def u_index(k, s):
        return LEADS + 2 * s + k

    for k in range(2):
        @pl.when(root & (core == k))
        def _():
            for s in range(8):
                for c in tile_load(s, buf.at[item_rows(u_index(k, s))], load_sem.at[s]):
                    c.start()

    barrier = pltpu.get_barrier_semaphore()
    peers = [device(y, z, other, x), device(y, z, core, x + 1), device(y, z, core, x + 3)]
    for dy, dz in ((1, 0), (3, 0), (0, 1), (0, 3)):
        for c in range(2):
            peers.append(device(y + dy, z + dz, c, x))
    for peer in peers:
        pl.semaphore_signal(barrier, inc=1, device_id=peer, device_id_type=MESH)
    pl.semaphore_wait(barrier, len(peers))

    def x_copy(k, part, slot, dx):
        rows = pl.ds(Q * part, Q)
        return pltpu.make_async_remote_copy(
            src_ref=ap.at[k, rows], dst_ref=ap.at[k, rows],
            send_sem=x_send.at[k, part, slot], recv_sem=x_recv.at[k, part],
            device_id=device(y, z, core, x + dx), device_id_type=MESH)

    for k in range(2):
        @pl.when(x == k)
        def _():
            for c in tile_load(0, ap.at[k], load_sem.at[8]):
                c.wait()
            for part in range(4):
                x_copy(k, part, 0, 1).start()
                x_copy(k, part, 1, 3).start()

    def tree_copy(t, n, slot, dy, dz, src=None):
        rows = pl.ds(n * NB + t * Q, Q)
        return pltpu.make_async_remote_copy(
            src_ref=buf.at[rows] if src is None else src.at[pl.ds(t * Q, Q)],
            dst_ref=buf.at[rows],
            send_sem=t_send.at[t, slot], recv_sem=t_recv.at[t, n],
            device_id=device(y + dy, z + dz, t % 2, x), device_id_type=MESH)

    def pair_copy(t, n, src=None):
        rows = pl.ds(n * NB + t * Q, Q)
        return pltpu.make_async_remote_copy(
            src_ref=buf.at[rows] if src is None else src.at[pl.ds(t * Q, Q)],
            dst_ref=buf.at[rows],
            send_sem=p_send.at[t], recv_sem=t_recv.at[t, n],
            device_id=device(y, z, other, x), device_id_type=MESH)

    def x_wait_and_forward():
        for k in range(2):
            for part in range(4):
                far = part // 2
                @pl.when(x != k)
                def _():
                    x_copy(k, part, 0, 1).wait_recv()
                fwd = lax.rem(k + (1 if far == 0 else 3), 4)
                @pl.when(x == fwd)
                def _():
                    x_copy(k, part, 0, 1 if far == 0 else 3).start()

    x_wait_and_forward()

    for k in range(2):
        @pl.when(root & (core == k))
        def _():
            for n, item in enumerate(ITEMS):
                if item[0] == "L":
                    lead = item[1]
                    if (lead == 0) != (k == 0):
                        continue
                    src = ap.at[0 if lead < 2 else 1]
                    for t in range(4):
                        pair_copy(t, n, src).start()
                else:
                    if item[1] != k:
                        continue
                    src = None
                    for c in tile_load(item[2], buf.at[item_rows(n)], load_sem.at[item[2]]):
                        c.wait()
                for t in range(4):
                    (_, dy, dz), _b, _c = children(t, y, z)
                    tree_copy(t, n, 0, dy, dz, src).start()

    def relay(n, _):
        for t in range(4):
            @pl.when(jnp.logical_not(root) & (core == t % 2))
            def _():
                tree_copy(t, n, 0, 0, 1).wait_recv()
                for slot, (cond, dy, dz) in enumerate(children(t, y, z)):
                    @pl.when(cond)
                    def _():
                        tree_copy(t, n, slot, dy, dz).start()
                pair_copy(t, n).start()
        return 0

    def out_copy(n, src):
        return pltpu.make_async_copy(src, out.at[item_rows(n)], out_sem.at[n])

    def drain(n, _):
        for t in range(4):
            @pl.when(jnp.logical_not(root) & (core != t % 2))
            def _():
                pair_copy(t, n).wait_recv()
        @pl.when(jnp.logical_not(root))
        def _():
            out_copy(n, buf.at[item_rows(n)]).start()
        return 0

    def both(n, _):
        relay(n, 0)
        drain(n - 2, 0)
        return 0

    relay(0, 0)
    relay(1, 0)
    lax.fori_loop(2, NITEM, both, 0)
    drain(NITEM - 2, 0)
    drain(NITEM - 1, 0)

    for k in range(2):
        @pl.when(root & (core == k))
        def _():
            for n in range(LEADS):
                if (n == 0) == (k == 0):
                    out_copy(n, ap.at[0 if n < 2 else 1]).start()
                else:
                    for t in range(4):
                        pair_copy(t, n).wait_recv()
                    out_copy(n, buf.at[item_rows(n)]).start()
            for n in range(LEADS):
                out_copy(n, buf.at[item_rows(n)]).wait()

    ap_copy = pltpu.make_async_copy(ap, ap_out, out_sem.at[NITEM])
    ap_copy.start()

    for k in range(2):
        for part in range(4):
            far = part // 2
            fwd = lax.rem(k + (1 if far == 0 else 3), 4)
            @pl.when(x == k)
            def _():
                x_copy(k, part, 0, 1).wait_send()
                x_copy(k, part, 1, 3).wait_send()
            @pl.when(x == fwd)
            def _():
                x_copy(k, part, 0, 1).wait_send()

    def sent(sem, count):
        rows = pl.ds(0, count * Q)
        pltpu.make_async_remote_copy(
            src_ref=buf.at[rows], dst_ref=buf.at[rows], send_sem=sem, recv_sem=t_recv.at[0, 0],
            device_id=device(y, z, other, x), device_id_type=MESH).wait_send()

    for t in range(4):
        @pl.when(jnp.logical_not(root) & (core == t % 2))
        def _():
            for slot, (cond, dy, dz) in enumerate(children(t, y, z)):
                @pl.when(cond)
                def _():
                    sent(t_send.at[t, slot], NITEM)
            sent(p_send.at[t], NITEM)
        for k in range(2):
            @pl.when(root & (core == k))
            def _():
                mine = (1 if k == 0 else 2)
                sent(t_send.at[t, 0], mine + 8)
                sent(p_send.at[t], mine)

    @pl.when(jnp.logical_not(root))
    def _():
        def done(n, _):
            out_copy(n, buf.at[item_rows(n)]).wait()
            return 0
        lax.fori_loop(0, NITEM, done, 0)
    ap_copy.wait()


def gather(mat):
    return pl.pallas_call(
        comm_kernel,
        out_shape=(jax.ShapeDtypeStruct((NITEM * NB, NB), F32), jax.ShapeDtypeStruct((2, NB, NB), F32)),
        in_specs=[pl.BlockSpec(memory_space=pl.ANY)],
        out_specs=(pl.BlockSpec(memory_space=pl.ANY), pl.BlockSpec(memory_space=pl.ANY)),
        scratch_shapes=[
            pltpu.VMEM((NITEM * NB, NB), F32),
            pltpu.VMEM((2, NB, NB), F32),
            pltpu.SemaphoreType.DMA((9, 4)),
            pltpu.SemaphoreType.DMA((2, 4, 2)),
            pltpu.SemaphoreType.DMA((2, 4)),
            pltpu.SemaphoreType.DMA((1,)),
            pltpu.SemaphoreType.DMA((4, 3)),
            pltpu.SemaphoreType.DMA((4, NITEM)),
            pltpu.SemaphoreType.DMA((4,)),
            pltpu.SemaphoreType.DMA((NITEM + 1,)),
        ],
        compiler_params=pltpu.CompilerParams(
            collective_id=0, has_side_effects=True, vmem_limit_bytes=60 * 1024 * 1024),
    )(mat)


def small_kernel(lead, ap, w_out, c_out, m0, m1):
    core, y, z, x = place()
    p = lax.axis_index("row")
    eye = jnp.where(
        lax.broadcasted_iota(jnp.int32, (NB, NB), 0) == lax.broadcasted_iota(jnp.int32, (NB, NB), 1), 1.0, 0.0
    ).astype(F32)
    m0[0:NB, :] = lead[0:NB, :]
    m0[NB:, :] = eye
    factor_tile(m0)
    inv0 = split(m0[NB:, :])
    l10 = dot3(split(lead[NB:2 * NB, :]), inv0, NN)
    l10s = split(l10)
    m1[0:NB, :] = lead[2 * NB:3 * NB, :] - dot3(l10s, l10s, NT)
    m1[NB:, :] = eye
    factor_tile(m1)
    inv1 = split(m1[NB:, :])
    x0 = dot3(split(ap[0]), inv0, NN)
    x1 = dot3(split(ap[1] - dot3(split(x0), l10s, NT)), inv1, NN)
    v = dot3(split(x1), inv1, NT)
    w0 = dot3(split(x0 - dot3(split(v), l10s, NN)), inv0, NT)
    for k, val in ((0, w0), (1, v)):
        h, l = split(val)
        w_out[0, :, k * NB:(k + 1) * NB] = h
        w_out[1, :, k * NB:(k + 1) * NB] = l
    first = jnp.where(p == 0, m0[0:NB, :], jnp.where(p == 1, l10, x0))
    second = jnp.where(p == 0, 0.0, jnp.where(p == 1, m1[0:NB, :], x1))
    c_out[...] = jnp.where(x == 0, first, second)


def small(lead, ap):
    return pl.pallas_call(
        small_kernel,
        out_shape=(jax.ShapeDtypeStruct((2, NB, 2 * NB), BF), jax.ShapeDtypeStruct((NB, NB), F32)),
        in_specs=[pl.BlockSpec((3 * NB, NB), lambda i: (0, 0)), pl.BlockSpec((2, NB, NB), lambda i: (0, 0, 0))],
        out_specs=(pl.BlockSpec((2, NB, 2 * NB), lambda i: (0, 0, 0)), pl.BlockSpec((NB, NB), lambda i: (0, 0))),
        grid=(1,),
        scratch_shapes=[pltpu.VMEM((2 * NB, NB), F32), pltpu.VMEM((2 * NB, NB), F32)],
        compiler_params=pltpu.CompilerParams(vmem_limit_bytes=60 * 1024 * 1024),
    )(lead, ap)


def trail_kernel(mat, g, w, c, out, sbuf, ubuf, obuf, s_sem, u_sem, o_sem):
    x = lax.axis_index("col")
    p = lax.axis_index("row")

    def s_copies(s):
        i = s % 2
        return [pltpu.make_async_copy(mat.at[:, 4 * s + b, 0, :], sbuf.at[i, :, pl.ds(128 * b, 128)], s_sem.at[i, b])
                for b in range(4)]

    def u_copy(s):
        i = s % 2
        return pltpu.make_async_copy(g.at[pl.ds((LEADS + 2 * s) * NB, 2 * NB)], ubuf.at[i], u_sem.at[i])

    def o_copies(s):
        i = s % 2
        return [pltpu.make_async_copy(obuf.at[i, :, pl.ds(128 * b, 128)], out.at[:, 4 * s + b, 0, :], o_sem.at[i, b])
                for b in range(4)]

    def start(s):
        for cp in s_copies(s):
            cp.start()
        u_copy(s).start()

    start(0)
    start(1)
    for s in range(8):
        i = s % 2
        if s >= 2:
            for cp in o_copies(s - 2):
                cp.wait()
        for cp in s_copies(s):
            cp.wait()
        u_copy(s).wait()
        for h in range(2):
            cols = pl.ds(256 * h, 256)
            u = split(ubuf[i, :, cols])
            new = sbuf[i, :, cols] - dot3((w[0], w[1]), u, NN)
            new = jnp.where(p < 2, 0.0, new)
            if s == 0:
                new = jnp.where(x < 2, c[:, cols], new)
            obuf[i, :, cols] = new
        if s + 2 < 8:
            start(s + 2)
        for cp in o_copies(s):
            cp.start()
    for s in (6, 7):
        for cp in o_copies(s):
            cp.wait()


def trail(mat, g, w, c):
    vm = pl.BlockSpec(memory_space=pltpu.VMEM)
    hb = pl.BlockSpec(memory_space=pl.ANY)
    return pl.pallas_call(
        trail_kernel,
        out_shape=jax.ShapeDtypeStruct(mat.shape, F32),
        in_specs=[hb, hb, vm, vm],
        out_specs=hb,
        scratch_shapes=[
            pltpu.VMEM((2, NB, NB), F32), pltpu.VMEM((2, 2 * NB, NB), F32), pltpu.VMEM((2, NB, NB), F32),
            pltpu.SemaphoreType.DMA((2, 4)), pltpu.SemaphoreType.DMA((2,)), pltpu.SemaphoreType.DMA((2, 4)),
        ],
        compiler_params=pltpu.CompilerParams(vmem_limit_bytes=60 * 1024 * 1024),
    )(mat, g, w, c)


def shards(matrix):
    mat = matrix.reshape(NB, 32, 1, 128)
    g, ap = gather(mat)
    w, c = small(g, ap)
    return trail(mat, g, w, c).reshape(matrix.shape)


def solution(mesh):
    spec = P(None, "row", None, None, "col", None)
    return jax.shard_map(shards, mesh=mesh, in_specs=(spec,), out_specs=spec, check_vma=False)
```

time: 947 us -> 569 us (0.60)
  the two profiles are of different devices: /device:TPU:47 before, /device:TPU:127 now
where the time goes in v1:
time: 569 us
  Pallas kernels  569 us (100%)
    pallas_call x1, Pallas kernels, gather(): pl.pallas_call(comm_kernel, out_shape=(jax.ShapeDtypeStruct((NITEM * NB,...  484 us
    pallas_call x1, Pallas kernels, small(): pl.pallas_call(small_kernel, out_shape=(jax.ShapeDtypeStruct((2, NB, 2 *...  62.6 us
    pallas_call x1, Pallas kernels, trail(): pl.pallas_call(trail_kernel, out_shape=jax.ShapeDtypeStruct(mat.shape, F3...  21.4 us

profile of v1, /device:TPU:127, one launch (start us, length us, event | category | flops | bytes accessed | tf_op | source)
XLA Modules:
  0.0 568.7 jit_solution(11152701902010488919)
XLA Ops:
  0.0 484.5 %shard_map.17 = (f32[9728,512]{1,0:T(8,128)}, f32[2,512,512]{2,1,0:T(8,128)}) custom-call(f32[512,32,1,128]{3,2,1,0:T(1,128)} %bitcast.2), custom_call_target="tpu_custom_call" | custom-call | tf_op jit(solution)/shard_map/pallas_call | solution.py:327
  484.5 62.6 %shard_map.18 = (bf16[2,512,1024]{2,1,0:T(8,128)(2,1)}, f32[512,512]{1,0:T(8,128)}) custom-call(f32[9728,512]{1,0:T(8,128)} %get-tuple-element.9.lead.g, f32[2,512,512]{2,1,0:T(8,128)} %get-tuple-element.10.ap), custom_call_target="tpu_custom_call" | custom-call | tf_op jit(solution)/shard_map/pallas_call | solution.py:379
  547.1 21.4 %shard_map.19 = f32[512,32,1,128]{3,2,1,0:T(1,128)} custom-call(f32[512,32,1,128]{3,2,1,0:T(1,128)} %bitcast.3, f32[9728,512]{1,0:T(8,128)} %get-tuple-element.9.lead.g, bf16[2,512,1024]{2,1,0:T(8,128)(2,1)} %get-tuple-element.11.w, f32[512,512]{1,0:T(8,128)} %get-tuple-element.12.c), custom_call_target="tpu_custom_call" | custom-call | tf_op jit(solution)/shard_map/pallas_call | solution.py:443

commit v2 on v1

v2 whole, which is shorter than its diff:
```python
import functools
import jax
import jax.numpy as jnp
from jax import lax
from jax.experimental import pallas as pl
from jax.experimental.pallas import tpu as pltpu
from jax.sharding import PartitionSpec as P

F32 = jnp.float32
BF = jnp.bfloat16
MESH = pl.DeviceIdType.MESH
NT = (((1,), (1,)), ((), ()))
NN = (((1,), (0,)), ((), ()))
NB = 512
Q = 128


def split(x):
    h=x.astype(BF)
    return h,(x-h.astype(F32)).astype(BF)

def dot3(a,b,dims):
    ah,al=a; bh,bl=b
    d=functools.partial(lax.dot_general,dimension_numbers=dims,preferred_element_type=F32)
    return d(ah,bh)+d(ah,bl)+d(al,bh)

def factor128(D):
    D3 = [D[8 * i:8 * i + 8, :] for i in range(16)]
    lane = lax.broadcasted_iota(jnp.int32, (8, 128), 1)
    sub = lax.broadcasted_iota(jnp.int32, (8, 128), 0)
    E3 = [jnp.where(lane == sub + 8 * i, 1.0, 0.0).astype(F32) for i in range(16)]
    zero = jnp.zeros((8, 128), F32)

    def bs(x, k):
        return jnp.take_along_axis(x, jnp.full((8, 128), k, jnp.int32), axis=0)

    U = [None] * 16
    for b in range(16):
        c = 8 * b
        B = {}
        for i in range(b, 16):
            for k in range(8):
                B[i, k] = jnp.broadcast_to(D3[i][:, c + k:c + k + 1], (8, 128))
        g = {(k, m): bs(B[b, m], k) for m in range(8) for k in range(m, 8)}
        r = [None] * 8
        s = {}
        for m in range(8):
            r[m] = lax.rsqrt(g[m, m])
            for k in range(m + 1, 8):
                s[k, m] = g[k, m] * r[m]
            for l in range(m + 1, 8):
                for k in range(l, 8):
                    g[k, l] = g[k, l] - s[k, m] * s[l, m]
        urow, erow = [], []
        for i in range(b, 16):
            mk = []
            for k in range(8):
                v = B[i, k]
                for m in range(k):
                    v = v - mk[m] * s[k, m]
                mk.append(v * r[k])
            d, e = D3[i], E3[i]
            if i == b:
                ou, oe = zero, zero
                for k in range(8):
                    u, w = bs(d, k) * r[k], bs(e, k) * r[k]
                    urow.append(u)
                    erow.append(w)
                    ou, oe = jnp.where(sub == k, u, ou), jnp.where(sub == k, w, oe)
                    if k < 7:
                        mm = jnp.where(sub > k, mk[k], 0.0)
                        d, e = d - mm * u, e - mm * w
                U[b] = jnp.where(lane >= sub + c, ou, 0.0)
                E3[b] = oe
            else:
                for k in range(8):
                    d, e = d - mk[k] * urow[k], e - mk[k] * erow[k]
                D3[i], E3[i] = d, e
    return jnp.concatenate(U, 0), jnp.concatenate(E3, 0)


def factor_tile(M):
    row = lax.broadcasted_iota(jnp.int32, (512, 128), 0)

    def body(k, _):
        c0 = pl.multiple_of(k * 128, 128)
        cols = pl.ds(c0, 128)
        U, Linv = factor128(M[cols, cols])
        live = pl.ds(pl.multiple_of(c0 + 128, 128), 512)
        X = dot3(split(M[live, cols]), split(Linv), NT)
        M[live, cols] = X
        M[cols, cols] = U.T
        lead = split(jnp.where(row >= c0 + 128, M[0:512, cols], 0.0))
        M[0:512, cols] = jnp.where(row >= c0, M[0:512, cols], 0.0)
        xh, xl = split(X)
        for h in range(2):
            r = slice(256 * h, 256 * h + 256)
            part = pl.ds(pl.multiple_of(c0 + 128 + 256 * h, 128), 256)
            M[part, :] -= dot3((xh[r], xl[r]), lead, NT)
        return 0

    lax.fori_loop(0, 4, body, 0)

LEADS = 3
NITEM = LEADS + 16
ORDER = [3, 4, 0, 5, 6, 1, 2] + list(range(7, NITEM))
DEEP = 6
PIECES = 2
R = Q // PIECES


def place():
    row = lax.axis_index("row")
    return lax.rem(row, 2), lax.rem(row // 2, 4), row // 8, lax.axis_index("col")


def device(y, z, core, x):
    return ((lax.rem(z + 4, 4) * 4 + lax.rem(y + 4, 4)) * 2 + core, lax.rem(x + 4, 4))


def to_tree(t, y, z):
    if t == 0:
        return y, z
    if t == 1:
        return lax.rem(4 - y, 4), lax.rem(4 - z, 4)
    if t == 2:
        return z, y
    return lax.rem(4 - z, 4), lax.rem(4 - y, 4)


def depth(t, y, z):
    u, v = to_tree(t, y, z)
    return jnp.where((u == 0) & (v > 0), 2 + v, u + v)


def at_step(i):
    head = jnp.where(i < 2, i + 3, jnp.where(i < 3, 0, jnp.where(i < 5, i + 2, i - 4)))
    return jnp.where(i < 7, head, i)


def children(t, y, z):
    u, v = to_tree(t, y, z)
    steps = {0: ((1, 0), (0, 1)), 1: ((-1, 0), (0, -1)), 2: ((0, 1), (1, 0)), 3: ((0, -1), (-1, 0))}
    (uy, uz), (vy, vz) = steps[t]
    return (
        ((v == 0) & (u < 3), uy, uz),
        ((u >= 1) & (v < 3), vy, vz),
        ((u == 1) & (v >= 1), -uy, -uz),
    )


def front_kernel(mat, out, w_out, c_out, buf, ap, m0, m1, wbuf, cbuf,
                 load_sem, x_send, x_recv, t_send, t_recv, p_send, lead_recv, u_recv, out_sem, w_sem, w_recv):
    core, y, z, x = place()
    root = (y == 0) & (z == 0)
    inner = jnp.logical_not(root)
    other = 1 - core

    def tile_load(s, dst, sem):
        return [
            pltpu.make_async_copy(mat.at[:, 4 * s + b, 0, :], dst.at[:, pl.ds(128 * b, 128)], sem.at[b])
            for b in range(4)
        ]

    def item_rows(n):
        return pl.ds(n * NB, NB)

    def item(k, s):
        return LEADS + 2 * s + k

    for k in range(2):
        for c in range(2):
            @pl.when((x == k) & (core == c))
            def _():
                for cp in tile_load(0, ap.at[c, k], load_sem.at[8]):
                    cp.start()
    for k in range(2):
        @pl.when(root & (core == k))
        def _():
            for s in range(8):
                for cp in tile_load(s, buf.at[item_rows(item(k, s))], load_sem.at[s]):
                    cp.start()

    barrier = pltpu.get_barrier_semaphore()
    peers = [device(y, z, other, x)]
    for c in range(2):
        peers += [device(y, z, c, x + 1), device(y, z, c, x + 3)]
        for dy, dz in ((1, 0), (3, 0), (0, 1), (0, 3)):
            peers.append(device(y + dy, z + dz, c, x))
    for peer in peers:
        pl.semaphore_signal(barrier, inc=1, device_id=peer, device_id_type=MESH)
    pl.semaphore_wait(barrier, len(peers))

    def x_copy(c, k, part, slot, dx):
        rows = pl.ds(Q * part, Q)
        return pltpu.make_async_remote_copy(
            src_ref=ap.at[c, k, rows], dst_ref=ap.at[c, k, rows],
            send_sem=x_send.at[c, k, part, slot], recv_sem=x_recv.at[c, k, part],
            device_id=device(y, z, 0, x + dx), device_id_type=MESH)

    for k in range(2):
        for c in range(2):
            @pl.when((x == k) & (core == c))
            def _():
                for cp in tile_load(0, ap.at[c, k], load_sem.at[8]):
                    cp.wait()
                for part in range(4):
                    x_copy(c, k, part, 0, 1).start()
                    x_copy(c, k, 3 - part, 1, 3).start()
                if c == 1:
                    for part in range(4):
                        x_copy(c, k, part, 2, 0).start()

    def x_far(k, part):
        return lax.rem(k + (1 if part < 2 else 3), 4), (1 if part < 2 else 3)

    def x_wait(c, k, part):
        x_copy(c, k, part, 0, 1).wait_recv()

    def x_forward(c, k):
        for part in (0, 3, 1, 2):
            fwd, dx = x_far(k, part)
            @pl.when(x == fwd)
            def _():
                x_wait(c, k, part)
                x_copy(c, k, part, 0, dx).start()

    def x_rest(c, k, part):
        fwd, _dx = x_far(k, part)
        away = (x != fwd) if c == 1 else (x != k) & (x != fwd)
        @pl.when(away)
        def _():
            x_wait(c, k, part)

    def piece(t, n, h):
        return pl.ds(pl.multiple_of(n * NB + t * Q + h * R, 8), R)

    def tree_copy(t, n, h, slot, dy, dz, src=None):
        rows = piece(t, n, h)
        return pltpu.make_async_remote_copy(
            src_ref=buf.at[rows] if src is None else src.at[pl.ds(t * Q + h * R, R)],
            dst_ref=buf.at[rows],
            send_sem=t_send.at[t, slot], recv_sem=t_recv.at[t, n * PIECES + h],
            device_id=device(y + dy, z + dz, 1, x), device_id_type=MESH)

    def lead_copy(t, n, h):
        rows = piece(t, n, h)
        return pltpu.make_async_remote_copy(
            src_ref=buf.at[rows], dst_ref=buf.at[rows],
            send_sem=p_send.at[t], recv_sem=lead_recv.at[n],
            device_id=device(y, z, other, x), device_id_type=MESH)

    def out_piece(t, n, h):
        return pl.ds(pl.multiple_of((n - LEADS) * NB + t * Q + h * R, 8), R)

    def u_copy(t, n, h):
        return pltpu.make_async_remote_copy(
            src_ref=buf.at[piece(t, n, h)], dst_ref=out.at[out_piece(t, n, h)],
            send_sem=p_send.at[t], recv_sem=u_recv.at[n - LEADS],
            device_id=device(y, z, other, x), device_id_type=MESH)

    def own_copy(t, n, h):
        return pltpu.make_async_copy(buf.at[piece(t, n, h)], out.at[out_piece(t, n, h)], out_sem.at[n - LEADS])

    for k in range(2):
        @pl.when(root & (core == k))
        def _():
            for n in ORDER:
                if n < LEADS:
                    if k == 1:
                        continue
                    c, kk = ((0, 0), (1, 0), (1, 1))[n]
                    src = ap.at[c, kk]
                    x_forward(c, kk)
                else:
                    if (n - LEADS) % 2 != k:
                        continue
                    c, src = None, None
                    s = (n - LEADS) // 2
                    for cp in tile_load(s, buf.at[item_rows(n)], load_sem.at[s]):
                        cp.wait()
                for t in range(4):
                    if c is not None:
                        x_rest(c, kk, t)
                    (_, dy, dz), _b, _c = children(t, y, z)
                    for h in range(PIECES):
                        tree_copy(t, n, h, 0, dy, dz, src).start()
            if k == 0:
                x_forward(0, 1)

    @pl.when(inner & (core == 0))
    def _():
        for k in range(2):
            for c in range(2):
                x_forward(c, k)

    skews = [(7 * depth(t, y, z)) // 3 for t in range(4)]
    LAST = (7 * DEEP) // 3

    def relay(step, _):
        for t in range(4):
            i = step - skews[t]
            @pl.when((i >= 0) & (i < PIECES * NITEM))
            def _():
                n, h = at_step(i // PIECES), lax.rem(i, PIECES)
                tree_copy(t, n, h, 0, 0, 1).wait_recv()
                for slot, (cond, dy, dz) in enumerate(children(t, y, z)):
                    @pl.when(cond)
                    def _():
                        tree_copy(t, n, h, slot, dy, dz).start()
                @pl.when(n < LEADS)
                def _():
                    lead_copy(t, n, h).start()
                @pl.when(n >= LEADS)
                def _():
                    u_copy(t, n, h).start()
                    own_copy(t, n, h).start()
        return 0

    @pl.when(inner & (core == 1))
    def _():
        lax.fori_loop(0, PIECES * NITEM + LAST, relay, 0)

    def lead_wait(n):
        rows = item_rows(n)
        pltpu.make_async_remote_copy(
            src_ref=buf.at[rows], dst_ref=buf.at[rows], send_sem=p_send.at[0], recv_sem=lead_recv.at[n],
            device_id=device(y, z, other, x), device_id_type=MESH).wait_recv()

    def lead_into(dst, n):
        c, k = ((0, 0), (1, 0), (1, 1))[n]
        @pl.when(root)
        def _():
            dst[0:NB, :] = ap[c, k]
        @pl.when(inner)
        def _():
            lead_wait(n)
            dst[0:NB, :] = buf[n * NB:(n + 1) * NB, :]

    @pl.when(core == 0)
    def _():
        eye = jnp.where(
            lax.broadcasted_iota(jnp.int32, (NB, NB), 0) == lax.broadcasted_iota(jnp.int32, (NB, NB), 1), 1.0, 0.0
        ).astype(F32)
        lead_into(m0, 0)
        m0[NB:, :] = eye
        factor_tile(m0)
        inv0 = split(m0[NB:, :])
        lead_into(cbuf.at[0], 1)
        l10 = dot3(split(cbuf[0]), inv0, NN)
        cbuf[0] = l10
        l10s = split(l10)
        lead_into(m1, 2)
        m1[0:NB, :] -= dot3(l10s, l10s, NT)
        m1[NB:, :] = eye
        factor_tile(m1)
        for k in range(2):
            for part in range(4):
                for c in range(2):
                    fwd, _dx = x_far(k, part)
                    here = (x == k) if c == 0 else (x < 0)
                    taken = here | (x == fwd) if (c, k) == (0, 1) else here | (x == fwd) | root
                    @pl.when(jnp.logical_not(taken))
                    def _():
                        x_wait(c, k, part)
        inv0, inv1 = split(m0[NB:, :]), split(m1[NB:, :])
        l10s = split(cbuf[0])
        for c in (1, 0):
            x0 = dot3(split(ap[c, 0]), inv0, NN)
            x1 = dot3(split(ap[c, 1] - dot3(split(x0), l10s, NT)), inv1, NN)
            v = dot3(split(x1), inv1, NT)
            wbuf[c, :, NB:] = v
            wbuf[c, :, :NB] = dot3(split(x0 - dot3(split(v), l10s, NN)), inv0, NT)
            if c == 1:
                first = jnp.where(root, cbuf[0], x0)
                second = jnp.where(root, m1[0:NB, :], x1)
            else:
                first = jnp.where(root, m0[0:NB, :], x0)
                second = jnp.where(root, 0.0, x1)
            cbuf[c] = jnp.where(x == 0, first, second)

    def results():
        pair = device(y, z, other, x)
        return [
            pltpu.make_async_remote_copy(
                src_ref=src, dst_ref=dst, send_sem=w_sem.at[i], recv_sem=w_recv.at[i],
                device_id=pair, device_id_type=MESH)
            for i, (src, dst) in enumerate(((wbuf.at[1], w_out), (cbuf.at[1], c_out)))
        ]

    @pl.when(core == 0)
    def _():
        own = [pltpu.make_async_copy(wbuf.at[0], w_out, w_sem.at[2]),
               pltpu.make_async_copy(cbuf.at[0], c_out, w_sem.at[3])]
        for cp in results() + own:
            cp.start()
        for cp in results():
            cp.wait_send()
        for cp in own:
            cp.wait()
        @pl.when(inner)
        def _():
            for i in range(16):
                rows = pl.ds(i * NB, NB)
                pltpu.make_async_remote_copy(
                    src_ref=out.at[rows], dst_ref=out.at[rows], send_sem=p_send.at[0], recv_sem=u_recv.at[i],
                    device_id=device(y, z, other, x), device_id_type=MESH).wait_recv()

    @pl.when(core == 1)
    def _():
        @pl.when(inner)
        def _():
            for i in range(16):
                pltpu.make_async_copy(
                    buf.at[pl.ds((LEADS + i) * NB, NB)], out.at[pl.ds(i * NB, NB)], out_sem.at[i]).wait()
        for cp in results():
            cp.wait_recv()

    for c in range(2):
        for k in range(2):
            for part in range(4):
                fwd, _dx = x_far(k, part)
                @pl.when((x == k) & (core == c))
                def _():
                    x_copy(c, k, part, 0, 1).wait_send()
                    x_copy(c, k, part, 1, 3).wait_send()
                    if c == 1:
                        x_copy(c, k, part, 2, 0).wait_send()
                @pl.when((x == fwd) & (core == 0))
                def _():
                    x_copy(c, k, part, 0, 1).wait_send()

    def sent(sem, count):
        rows = pl.ds(0, count * Q)
        pltpu.make_async_remote_copy(
            src_ref=buf.at[rows], dst_ref=buf.at[rows], send_sem=sem, recv_sem=t_recv.at[0, 0],
            device_id=device(y, z, other, x), device_id_type=MESH).wait_send()

    for t in range(4):
        @pl.when(inner & (core == 1))
        def _():
            for slot, (cond, dy, dz) in enumerate(children(t, y, z)):
                @pl.when(cond)
                def _():
                    sent(t_send.at[t, slot], NITEM)
            sent(p_send.at[t], NITEM)
        for k in range(2):
            @pl.when(root & (core == k))
            def _():
                sent(t_send.at[t, 0], 8 + (LEADS if k == 0 else 0))


def front(mat):
    hb = pl.BlockSpec(memory_space=pl.ANY)
    dma = pltpu.SemaphoreType.DMA
    return pl.pallas_call(
        front_kernel,
        out_shape=(
            jax.ShapeDtypeStruct((16 * NB, NB), F32),
            jax.ShapeDtypeStruct((NB, 2 * NB), F32),
            jax.ShapeDtypeStruct((NB, NB), F32),
        ),
        in_specs=[hb],
        out_specs=(hb, hb, hb),
        scratch_shapes=[
            pltpu.VMEM((NITEM * NB, NB), F32),
            pltpu.VMEM((2, 2, NB, NB), F32),
            pltpu.VMEM((2 * NB, NB), F32),
            pltpu.VMEM((2 * NB, NB), F32),
            pltpu.VMEM((2, NB, 2 * NB), F32),
            pltpu.VMEM((2, NB, NB), F32),
            dma((9, 4)), dma((2, 2, 4, 3)), dma((2, 2, 4)), dma((4, 3)), dma((4, NITEM * PIECES)),
            dma((4,)), dma((LEADS,)), dma((16,)), dma((16,)), dma((4,)), dma((2,)),
        ],
        compiler_params=pltpu.CompilerParams(
            collective_id=0, has_side_effects=True, vmem_limit_bytes=63 * 1024 * 1024),
    )(mat)


def trail_kernel(mat, g, w, c, out, whl, sbuf, ubuf, obuf, s_sem, u_sem, o_sem):
    x = lax.axis_index("col")
    p = lax.axis_index("row")

    def s_copies(s):
        i = s % 2
        return [pltpu.make_async_copy(mat.at[:, 4 * s + b, 0, :], sbuf.at[i, :, pl.ds(128 * b, 128)], s_sem.at[i, b])
                for b in range(4)]

    def u_copy(s):
        i = s % 2
        return pltpu.make_async_copy(g.at[pl.ds(2 * s * NB, 2 * NB)], ubuf.at[i], u_sem.at[i])

    def o_copies(s):
        i = s % 2
        return [pltpu.make_async_copy(obuf.at[i, :, pl.ds(128 * b, 128)], out.at[:, 4 * s + b, 0, :], o_sem.at[i, b])
                for b in range(4)]

    def start(s):
        for cp in s_copies(s):
            cp.start()
        u_copy(s).start()

    start(0)
    start(1)
    whl[0], whl[1] = split(w[...])
    for s in range(8):
        i = s % 2
        if s >= 2:
            for cp in o_copies(s - 2):
                cp.wait()
        for cp in s_copies(s):
            cp.wait()
        u_copy(s).wait()
        for h in range(2):
            cols = pl.ds(256 * h, 256)
            u = split(ubuf[i, :, cols])
            new = sbuf[i, :, cols] - dot3((whl[0], whl[1]), u, NN)
            new = jnp.where(p < 2, 0.0, new)
            if s == 0:
                new = jnp.where(x < 2, c[:, cols], new)
            obuf[i, :, cols] = new
        if s + 2 < 8:
            start(s + 2)
        for cp in o_copies(s):
            cp.start()
    for s in (6, 7):
        for cp in o_copies(s):
            cp.wait()


def trail(mat, g, w, c):
    vm = pl.BlockSpec(memory_space=pltpu.VMEM)
    hb = pl.BlockSpec(memory_space=pl.ANY)
    return pl.pallas_call(
        trail_kernel,
        out_shape=jax.ShapeDtypeStruct(mat.shape, F32),
        in_specs=[hb, hb, vm, vm],
        out_specs=hb,
        scratch_shapes=[
            pltpu.VMEM((2, NB, 2 * NB), BF),
            pltpu.VMEM((2, NB, NB), F32), pltpu.VMEM((2, 2 * NB, NB), F32), pltpu.VMEM((2, NB, NB), F32),
            pltpu.SemaphoreType.DMA((2, 4)), pltpu.SemaphoreType.DMA((2,)), pltpu.SemaphoreType.DMA((2, 4)),
        ],
        compiler_params=pltpu.CompilerParams(vmem_limit_bytes=60 * 1024 * 1024),
    )(mat, g, w, c)


def shards(matrix):
    mat = matrix.reshape(NB, 32, 1, 128)
    u, w, c = front(mat)
    return trail(mat, u, w, c).reshape(matrix.shape)


def solution(mesh):
    spec = P(None, "row", None, None, "col", None)
    return jax.shard_map(shards, mesh=mesh, in_specs=(spec,), out_specs=spec, check_vma=False)
```

time: 569 us -> 137 us (0.24)
  the two profiles are of different devices: /device:TPU:127 before, /device:TPU:47 now
where the time goes in v2:
time: 137 us; the launch traced here: 136 us
  Pallas kernels  136 us (99%)
    pallas_call x1, Pallas kernels, front(): pl.pallas_call(front_kernel, out_shape=(jax.ShapeDtypeStruct((16 * NB, NB...  115 us
    pallas_call x1, Pallas kernels, trail(): pl.pallas_call(trail_kernel, out_shape=jax.ShapeDtypeStruct(mat.shape, F3...  21.4 us

profile of v2, /device:TPU:47, one launch (start us, length us, event | category | flops | bytes accessed | tf_op | source)
XLA Modules:
  0.0 136.4 jit_solution(3638029468191532338)
XLA Ops:
  0.0 114.7 %shard_map.17 = (f32[8192,512]{1,0:T(8,128)}, f32[512,1024]{1,0:T(8,128)}, f32[512,512]{1,0:T(8,128)}) custom-call(f32[512,32,1,128]{3,2,1,0:T(1,128)} %bitcast.2), custom_call_target="tpu_custom_call" | custom-call | tf_op jit(solution)/shard_map/pallas_call | solution.py:456
  114.7 21.4 %shard_map.18 = f32[512,32,1,128]{3,2,1,0:T(1,128)} custom-call(f32[512,32,1,128]{3,2,1,0:T(1,128)} %bitcast.3, f32[8192,512]{1,0:T(8,128)} %get-tuple-element.8.g, f32[512,1024]{1,0:T(8,128)} %get-tuple-element.9.w, f32[512,512]{1,0:T(8,128)} %get-tuple-element.10.c), custom_call_target="tpu_custom_call" | custom-call | tf_op jit(solution)/shard_map/pallas_call | solution.py:534

commit v3 on v2

--- a/solution.py
+++ b/solution.py
@@ -103,9 +103,9 @@
 
 LEADS = 3
 NITEM = LEADS + 16
-ORDER = [3, 4, 0, 5, 6, 1, 2] + list(range(7, NITEM))
+ORDER = [3, 4, 5, 6, 0, 8, 7, 10, 9, 12, 11, 14, 1, 16, 2, 18, 13, 15, 17]
 DEEP = 6
-PIECES = 2
+PIECES = 4
 R = Q // PIECES
 
 
@@ -134,8 +134,10 @@
 
 
 def at_step(i):
-    head = jnp.where(i < 2, i + 3, jnp.where(i < 3, 0, jnp.where(i < 5, i + 2, i - 4)))
-    return jnp.where(i < 7, head, i)
+    j = i // 2
+    odd = 4 + 2 * j
+    even = jnp.where(j < 2, 3 + 2 * j, jnp.where(j < 3, 0, jnp.where(j < 6, 1 + 2 * j, jnp.where(j < 7, 1, 2))))
+    return jnp.where(i >= 16, 13 + 2 * (i - 16), jnp.where(lax.rem(i, 2) == 1, odd, even))
 
 
 def children(t, y, z):
@@ -149,8 +151,8 @@
     )
 
 
-def front_kernel(mat, out, w_out, c_out, buf, ap, m0, m1, wbuf, cbuf,
-                 load_sem, x_send, x_recv, t_send, t_recv, p_send, lead_recv, u_recv, out_sem, w_sem, w_recv):
+def front_kernel(mat, out, fac, ap_out, top, buf, ap, m0, m1, tmp,
+                 load_sem, pace, x_send, x_recv, t_send, t_recv, p_send, lead_recv, u_recv, out_sem, f_send, f_recv, f_own):
     core, y, z, x = place()
     root = (y == 0) & (z == 0)
     inner = jnp.logical_not(root)
@@ -204,12 +206,14 @@
             def _():
                 for cp in tile_load(0, ap.at[c, k], load_sem.at[8]):
                     cp.wait()
-                for part in range(4):
-                    x_copy(c, k, part, 0, 1).start()
-                    x_copy(c, k, 3 - part, 1, 3).start()
                 if c == 1:
                     for part in range(4):
                         x_copy(c, k, part, 2, 0).start()
+                @pl.when(inner if (c, k) != (0, 0) else core == 0)
+                def _():
+                    for part in range(4):
+                        x_copy(c, k, part, 0, 1).start()
+                        x_copy(c, k, 3 - part, 1, 3).start()
 
     def x_far(k, part):
         return lax.rem(k + (1 if part < 2 else 3), 4), (1 if part < 2 else 3)
@@ -225,10 +229,18 @@
                 x_wait(c, k, part)
                 x_copy(c, k, part, 0, dx).start()
 
-    def x_rest(c, k, part):
+    def root_send(k):
+        @pl.when(x == k)
+        def _():
+            for part in range(4):
+                x_wait(1, k, part)
+            for part in range(4):
+                x_copy(1, k, part, 0, 1).start()
+                x_copy(1, k, 3 - part, 1, 3).start()
+
+    def root_rest(c, k, part):
         fwd, _dx = x_far(k, part)
-        away = (x != fwd) if c == 1 else (x != k) & (x != fwd)
-        @pl.when(away)
+        @pl.when((x != k) & (x != fwd))
         def _():
             x_wait(c, k, part)
 
@@ -271,22 +283,31 @@
                         continue
                     c, kk = ((0, 0), (1, 0), (1, 1))[n]
                     src = ap.at[c, kk]
-                    x_forward(c, kk)
+                    if n == 1:
+                        x_forward(1, 0)
+                        x_forward(1, 1)
                 else:
                     if (n - LEADS) % 2 != k:
                         continue
                     c, src = None, None
                     s = (n - LEADS) // 2
+                    if k == 1 and s > 0:
+                        pl.semaphore_wait(pace, 1)
                     for cp in tile_load(s, buf.at[item_rows(n)], load_sem.at[s]):
                         cp.wait()
                 for t in range(4):
                     if c is not None:
-                        x_rest(c, kk, t)
+                        root_rest(c, kk, t)
                     (_, dy, dz), _b, _c = children(t, y, z)
                     for h in range(PIECES):
                         tree_copy(t, n, h, 0, dy, dz, src).start()
-            if k == 0:
-                x_forward(0, 1)
+                if k == 0 and n == 3:
+                    root_send(0)
+                if k == 0 and n == 5:
+                    x_forward(0, 0)
+                    root_send(1)
+                if k == 0 and n in ORDER[:14:2]:
+                    pl.semaphore_signal(pace, inc=1, device_id=device(y, z, other, x), device_id_type=MESH)
 
     @pl.when(inner & (core == 0))
     def _():
@@ -294,8 +315,8 @@
             for c in range(2):
                 x_forward(c, k)
 
-    skews = [(7 * depth(t, y, z)) // 3 for t in range(4)]
-    LAST = (7 * DEEP) // 3
+    skews = [4 * depth(t, y, z) for t in range(4)]
+    LAST = 4 * DEEP
 
     def relay(step, _):
         for t in range(4):
@@ -337,6 +358,24 @@
             lead_wait(n)
             dst[0:NB, :] = buf[n * NB:(n + 1) * NB, :]
 
+    def result(i, c):
+        return (
+            (ap.at[c, 0], ap_out.at[0]), (ap.at[c, 1], ap_out.at[1]),
+            (m0.at[pl.ds(NB, NB)], fac.at[0]), (tmp, fac.at[1]), (m1.at[pl.ds(NB, NB)], fac.at[2]),
+            (tmp, top), (m1.at[pl.ds(0, NB)], top),
+        )[i]
+
+    def hand(i):
+        src, dst = result(i, 1)
+        sem = min(i, 5)
+        return pltpu.make_async_remote_copy(
+            src_ref=src, dst_ref=dst, send_sem=f_send.at[sem], recv_sem=f_recv.at[sem],
+            device_id=device(y, z, other, x), device_id_type=MESH)
+
+    def keep(i):
+        src, dst = result(i, 0)
+        return pltpu.make_async_copy(src, dst, f_own.at[i])
+
     @pl.when(core == 0)
     def _():
         eye = jnp.where(
@@ -346,65 +385,51 @@
         m0[NB:, :] = eye
         factor_tile(m0)
         inv0 = split(m0[NB:, :])
-        lead_into(cbuf.at[0], 1)
-        l10 = dot3(split(cbuf[0]), inv0, NN)
-        cbuf[0] = l10
+        lead_into(tmp, 1)
+        l10 = dot3(split(tmp[...]), inv0, NN)
+        tmp[...] = l10
         l10s = split(l10)
         lead_into(m1, 2)
         m1[0:NB, :] -= dot3(l10s, l10s, NT)
         m1[NB:, :] = eye
-        factor_tile(m1)
         for k in range(2):
             for part in range(4):
                 for c in range(2):
                     fwd, _dx = x_far(k, part)
                     here = (x == k) if c == 0 else (x < 0)
-                    taken = here | (x == fwd) if (c, k) == (0, 1) else here | (x == fwd) | root
-                    @pl.when(jnp.logical_not(taken))
+                    @pl.when(jnp.logical_not(here | (x == fwd) | root))
                     def _():
                         x_wait(c, k, part)
-        inv0, inv1 = split(m0[NB:, :]), split(m1[NB:, :])
-        l10s = split(cbuf[0])
-        for c in (1, 0):
-            x0 = dot3(split(ap[c, 0]), inv0, NN)
-            x1 = dot3(split(ap[c, 1] - dot3(split(x0), l10s, NT)), inv1, NN)
-            v = dot3(split(x1), inv1, NT)
-            wbuf[c, :, NB:] = v
-            wbuf[c, :, :NB] = dot3(split(x0 - dot3(split(v), l10s, NN)), inv0, NT)
-            if c == 1:
-                first = jnp.where(root, cbuf[0], x0)
-                second = jnp.where(root, m1[0:NB, :], x1)
-            else:
-                first = jnp.where(root, m0[0:NB, :], x0)
-                second = jnp.where(root, 0.0, x1)
-            cbuf[c] = jnp.where(x == 0, first, second)
-
-    def results():
-        pair = device(y, z, other, x)
-        return [
+        for i in range(4):
+            hand(i).start()
+            keep(i).start()
+        factor_tile(m1)
+        hand(4).start()
+        keep(4).start()
+        @pl.when(root)
+        def _():
+            pltpu.make_async_copy(m0.at[pl.ds(0, NB)], top, f_own.at[5]).start()
+            @pl.when(x == 0)
+            def _():
+                hand(5).start()
+            @pl.when(x != 0)
+            def _():
+                hand(6).start()
+        for i in range(5):
+            hand(i).wait_send()
+            keep(i).wait()
+        @pl.when(root)
+        def _():
+            pltpu.make_async_copy(m0.at[pl.ds(0, NB)], top, f_own.at[5]).wait()
+            hand(5).wait_send()
+
+    @pl.when((core == 0) & inner)
+    def _():
+        for i in range(16):
+            rows = pl.ds(i * NB, NB)
             pltpu.make_async_remote_copy(
-                src_ref=src, dst_ref=dst, send_sem=w_sem.at[i], recv_sem=w_recv.at[i],
-                device_id=pair, device_id_type=MESH)
-            for i, (src, dst) in enumerate(((wbuf.at[1], w_out), (cbuf.at[1], c_out)))
-        ]
-
-    @pl.when(core == 0)
-    def _():
-        own = [pltpu.make_async_copy(wbuf.at[0], w_out, w_sem.at[2]),
-               pltpu.make_async_copy(cbuf.at[0], c_out, w_sem.at[3])]
-        for cp in results() + own:
-            cp.start()
-        for cp in results():
-            cp.wait_send()
-        for cp in own:
-            cp.wait()
-        @pl.when(inner)
-        def _():
-            for i in range(16):
-                rows = pl.ds(i * NB, NB)
-                pltpu.make_async_remote_copy(
-                    src_ref=out.at[rows], dst_ref=out.at[rows], send_sem=p_send.at[0], recv_sem=u_recv.at[i],
-                    device_id=device(y, z, other, x), device_id_type=MESH).wait_recv()
+                src_ref=out.at[rows], dst_ref=out.at[rows], send_sem=p_send.at[0], recv_sem=u_recv.at[i],
+                device_id=device(y, z, other, x), device_id_type=MESH).wait_recv()
 
     @pl.when(core == 1)
     def _():
@@ -413,20 +438,27 @@
             for i in range(16):
                 pltpu.make_async_copy(
                     buf.at[pl.ds((LEADS + i) * NB, NB)], out.at[pl.ds(i * NB, NB)], out_sem.at[i]).wait()
-        for cp in results():
-            cp.wait_recv()
+        for i in range(5):
+            hand(i).wait_recv()
+        @pl.when(root)
+        def _():
+            hand(5).wait_recv()
 
     for c in range(2):
         for k in range(2):
             for part in range(4):
                 fwd, _dx = x_far(k, part)
-                @pl.when((x == k) & (core == c))
+                sender = jnp.where(root, (core == 0) & ((c, k) != (0, 1)), core == c)
+                @pl.when((x == k) & sender)
                 def _():
                     x_copy(c, k, part, 0, 1).wait_send()
                     x_copy(c, k, part, 1, 3).wait_send()
-                    if c == 1:
+                if c == 1:
+                    @pl.when((x == k) & (core == 1))
+                    def _():
                         x_copy(c, k, part, 2, 0).wait_send()
-                @pl.when((x == fwd) & (core == 0))
+                passed = (x == fwd) & (core == 0)
+                @pl.when(passed & inner if (c, k) == (0, 1) else passed)
                 def _():
                     x_copy(c, k, part, 0, 1).wait_send()
 
@@ -457,98 +489,136 @@
         front_kernel,
         out_shape=(
             jax.ShapeDtypeStruct((16 * NB, NB), F32),
-            jax.ShapeDtypeStruct((NB, 2 * NB), F32),
+            jax.ShapeDtypeStruct((3, NB, NB), F32),
+            jax.ShapeDtypeStruct((2, NB, NB), F32),
             jax.ShapeDtypeStruct((NB, NB), F32),
         ),
         in_specs=[hb],
-        out_specs=(hb, hb, hb),
+        out_specs=(hb, hb, hb, hb),
         scratch_shapes=[
             pltpu.VMEM((NITEM * NB, NB), F32),
             pltpu.VMEM((2, 2, NB, NB), F32),
             pltpu.VMEM((2 * NB, NB), F32),
             pltpu.VMEM((2 * NB, NB), F32),
-            pltpu.VMEM((2, NB, 2 * NB), F32),
-            pltpu.VMEM((2, NB, NB), F32),
-            dma((9, 4)), dma((2, 2, 4, 3)), dma((2, 2, 4)), dma((4, 3)), dma((4, NITEM * PIECES)),
-            dma((4,)), dma((LEADS,)), dma((16,)), dma((16,)), dma((4,)), dma((2,)),
+            pltpu.VMEM((NB, NB), F32),
+            dma((9, 4)), pltpu.SemaphoreType.REGULAR, dma((2, 2, 4, 3)), dma((2, 2, 4)), dma((4, 3)), dma((4, NITEM * PIECES)),
+            dma((4,)), dma((LEADS,)), dma((16,)), dma((16,)), dma((6,)), dma((6,)), dma((6,)),
         ],
         compiler_params=pltpu.CompilerParams(
             collective_id=0, has_side_effects=True, vmem_limit_bytes=63 * 1024 * 1024),
     )(mat)
 
 
-def trail_kernel(mat, g, w, c, out, whl, sbuf, ubuf, obuf, s_sem, u_sem, o_sem):
+def tri(a, inv):
+    low = tuple(v[:, :256] for v in a)
+    return jnp.concatenate([
+        dot3(low, tuple(v[:256, :256] for v in inv), NN),
+        dot3(a, tuple(v[:, 256:] for v in inv), NN)], 1)
+
+
+def tri_t(a, inv):
+    high = tuple(v[:, 256:] for v in a)
+    return jnp.concatenate([
+        dot3(a, tuple(v[:256, :] for v in inv), NT),
+        dot3(high, tuple(v[256:, 256:] for v in inv), NT)], 1)
+
+
+def trail_kernel(mat, u, fac, ap, top, out, fv, av, tv, whl, sbuf, ubuf, obuf, f_sem, s_sem, u_sem, o_sem):
     x = lax.axis_index("col")
     p = lax.axis_index("row")
+    OUT = obuf.shape[0]
 
     def s_copies(s):
-        i = s % 2
-        return [pltpu.make_async_copy(mat.at[:, 4 * s + b, 0, :], sbuf.at[i, :, pl.ds(128 * b, 128)], s_sem.at[i, b])
+        return [pltpu.make_async_copy(mat.at[:, 4 * s + b, 0, :], sbuf.at[s, :, pl.ds(128 * b, 128)], s_sem.at[s, b])
                 for b in range(4)]
 
     def u_copy(s):
-        i = s % 2
-        return pltpu.make_async_copy(g.at[pl.ds(2 * s * NB, 2 * NB)], ubuf.at[i], u_sem.at[i])
+        return pltpu.make_async_copy(u.at[pl.ds(2 * s * NB, 2 * NB)], ubuf.at[s], u_sem.at[s])
 
     def o_copies(s):
-        i = s % 2
+        i = s % OUT
         return [pltpu.make_async_copy(obuf.at[i, :, pl.ds(128 * b, 128)], out.at[:, 4 * s + b, 0, :], o_sem.at[i, b])
                 for b in range(4)]
 
-    def start(s):
+    first = [
+        pltpu.make_async_copy(ap.at[0], av.at[0], f_sem.at[0]),
+        pltpu.make_async_copy(fac.at[0], fv.at[0], f_sem.at[1]),
+        pltpu.make_async_copy(ap.at[1], av.at[1], f_sem.at[2]),
+        pltpu.make_async_copy(fac.at[1], fv.at[1], f_sem.at[3]),
+        pltpu.make_async_copy(fac.at[2], fv.at[2], f_sem.at[4]),
+        pltpu.make_async_copy(top, tv, f_sem.at[5]),
+    ]
+    for cp in first:
+        cp.start()
+    for s in range(8):
+        u_copy(s).start()
         for cp in s_copies(s):
             cp.start()
-        u_copy(s).start()
-
-    start(0)
-    start(1)
-    whl[0], whl[1] = split(w[...])
+
+    first[0].wait()
+    first[1].wait()
+    inv0 = split(fv[0])
+    x0 = tri(split(av[0]), inv0)
+    first[2].wait()
+    first[3].wait()
+    l10 = split(fv[1])
+    rest = av[1] - dot3(split(x0), l10, NT)
+    first[4].wait()
+    inv1 = split(fv[2])
+    x1 = tri(split(rest), inv1)
+    v = tri_t(split(x1), inv1)
+    vs = split(v)
+    ws = split(tri_t(split(x0 - dot3(vs, l10, NN)), inv0))
+    for i in range(2):
+        whl[i, :, :NB] = ws[i]
+        whl[i, :, NB:] = vs[i]
+    first[5].wait()
+    own = jnp.where((p == 0) & (x > 0), 0.0, tv[...])
+    av[0] = jnp.where(p < 2, own, jnp.where(x == 0, x0, x1))
+
     for s in range(8):
-        i = s % 2
-        if s >= 2:
-            for cp in o_copies(s - 2):
+        if s >= OUT:
+            for cp in o_copies(s - OUT):
                 cp.wait()
+        u_copy(s).wait()
         for cp in s_copies(s):
             cp.wait()
-        u_copy(s).wait()
         for h in range(2):
             cols = pl.ds(256 * h, 256)
-            u = split(ubuf[i, :, cols])
-            new = sbuf[i, :, cols] - dot3((whl[0], whl[1]), u, NN)
+            part = split(ubuf[s, :, cols])
+            new = sbuf[s, :, cols] - dot3((whl[0], whl[1]), part, NN)
             new = jnp.where(p < 2, 0.0, new)
             if s == 0:
-                new = jnp.where(x < 2, c[:, cols], new)
-            obuf[i, :, cols] = new
-        if s + 2 < 8:
-            start(s + 2)
+                new = jnp.where(x < 2, av[0, :, cols], new)
+            obuf[s % OUT, :, cols] = new
         for cp in o_copies(s):
             cp.start()
-    for s in (6, 7):
+    for s in range(8 - OUT, 8):
         for cp in o_copies(s):
             cp.wait()
 
 
-def trail(mat, g, w, c):
-    vm = pl.BlockSpec(memory_space=pltpu.VMEM)
+def trail(mat, u, fac, ap, top):
     hb = pl.BlockSpec(memory_space=pl.ANY)
+    dma = pltpu.SemaphoreType.DMA
     return pl.pallas_call(
         trail_kernel,
         out_shape=jax.ShapeDtypeStruct(mat.shape, F32),
-        in_specs=[hb, hb, vm, vm],
+        in_specs=[hb] * 5,
         out_specs=hb,
         scratch_shapes=[
+            pltpu.VMEM((3, NB, NB), F32), pltpu.VMEM((2, NB, NB), F32), pltpu.VMEM((NB, NB), F32),
             pltpu.VMEM((2, NB, 2 * NB), BF),
-            pltpu.VMEM((2, NB, NB), F32), pltpu.VMEM((2, 2 * NB, NB), F32), pltpu.VMEM((2, NB, NB), F32),
-            pltpu.SemaphoreType.DMA((2, 4)), pltpu.SemaphoreType.DMA((2,)), pltpu.SemaphoreType.DMA((2, 4)),
+            pltpu.VMEM((8, NB, NB), F32), pltpu.VMEM((8, 2 * NB, NB), F32), pltpu.VMEM((3, NB, NB), F32),
+            dma((6,)), dma((8, 4)), dma((8,)), dma((3, 4)),
         ],
-        compiler_params=pltpu.CompilerParams(vmem_limit_bytes=60 * 1024 * 1024),
-    )(mat, g, w, c)
+        compiler_params=pltpu.CompilerParams(vmem_limit_bytes=63 * 1024 * 1024),
+    )(mat, u, fac, ap, top)
 
 
 def shards(matrix):
     mat = matrix.reshape(NB, 32, 1, 128)
-    u, w, c = front(mat)
-    return trail(mat, u, w, c).reshape(matrix.shape)
+    return trail(mat, *front(mat)).reshape(matrix.shape)
 
 
 def solution(mesh):

time: 137 us -> 120 us (0.88)
  Pallas kernels: 136 us -> 120 us
    pallas_call x1, Pallas kernels: 115 us -> 94.4 us  [front(): pl.pallas_call(front_kernel, out_shape=(jax.ShapeDtypeStruct((16 * NB, NB...]
    pallas_call x1, Pallas kernels: 21.4 us -> 25.6 us  [trail(): pl.pallas_call(trail_kernel, out_shape=jax.ShapeDtypeStruct(mat.shape, F3...]
where the time goes in v3:
time: 120 us
  Pallas kernels  120 us (100%)
    pallas_call x1, Pallas kernels, front(): pl.pallas_call(front_kernel, out_shape=(jax.ShapeDtypeStruct((16 * NB, NB...  94.4 us
    pallas_call x1, Pallas kernels, trail(): pl.pallas_call(trail_kernel, out_shape=jax.ShapeDtypeStruct(mat.shape, F3...  25.6 us

profile of v3, /device:TPU:47, one launch (start us, length us, event | category | flops | bytes accessed | tf_op | source)
XLA Modules:
  0.0 120.3 jit_solution(6622581732727116908)
XLA Ops:
  0.0 94.4 %shard_map.17 = (f32[8192,512]{1,0:T(8,128)}, f32[3,512,512]{2,1,0:T(8,128)}, f32[2,512,512]{2,1,0:T(8,128)}, f32[512,512]{1,0:T(8,128)}) custom-call(f32[512,32,1,128]{3,2,1,0:T(1,128)} %bitcast.2), custom_call_target="tpu_custom_call" | custom-call | tf_op jit(solution)/shard_map/pallas_call | solution.py:488
  94.5 25.6 %shard_map.18 = f32[512,32,1,128]{3,2,1,0:T(1,128)} custom-call(f32[512,32,1,128]{3,2,1,0:T(1,128)} %bitcast.3, f32[8192,512]{1,0:T(8,128)} %get-tuple-element.9.u, f32[3,512,512]{2,1,0:T(8,128)} %get-tuple-element.10.fac, f32[2,512,512]{2,1,0:T(8,128)} %get-tuple-element.11.ap, f32[512,512]{1,0:T(8,128)} %get-tuple-element.12.top), custom_call_target="tpu_custom_call" | custom-call | tf_op jit(solution)/shard_map/pallas_call | solution.py:604

commit v4 on v3

--- a/solution.py
+++ b/solution.py
@@ -90,22 +90,29 @@
         X = dot3(split(M[live, cols]), split(Linv), NT)
         M[live, cols] = X
         M[cols, cols] = U.T
-        lead = split(jnp.where(row >= c0 + 128, M[0:512, cols], 0.0))
-        M[0:512, cols] = jnp.where(row >= c0, M[0:512, cols], 0.0)
-        xh, xl = split(X)
-        for h in range(2):
-            r = slice(256 * h, 256 * h + 256)
-            part = pl.ds(pl.multiple_of(c0 + 128 + 256 * h, 128), 256)
-            M[part, :] -= dot3((xh[r], xl[r]), lead, NT)
+        below = M[0:512, cols]
+        M[0:512, cols] = jnp.where(row >= c0, below, 0.0)
+        xs = split(X)
+        for j in range(3):
+            @pl.when(k == j)
+            def _():
+                right = slice(128 * (j + 1), 512)
+                lead = split(below[right])
+                for h in range(2):
+                    r = slice(256 * h, 256 * h + 256)
+                    start = 128 * (j + 1) + 256 * h
+                    M[start:start + 256, right] -= dot3(tuple(v[r] for v in xs), lead, NT)
         return 0
 
     lax.fori_loop(0, 4, body, 0)
 
 LEADS = 3
 NITEM = LEADS + 16
-ORDER = [3, 4, 5, 6, 0, 8, 7, 10, 9, 12, 11, 14, 1, 16, 2, 18, 13, 15, 17]
+EVEN = [3, 5, 7, 1, 2, 9, 11, 13, 15, 17]
+ODD = [4, 6, 8, 10, 12, 14, 16, 18]
 DEEP = 6
 PIECES = 4
+GATE = 12
 R = Q // PIECES
 
 
@@ -133,11 +140,11 @@
     return jnp.where((u == 0) & (v > 0), 2 + v, u + v)
 
 
-def at_step(i):
+def at_step(i, x):
     j = i // 2
-    odd = 4 + 2 * j
-    even = jnp.where(j < 2, 3 + 2 * j, jnp.where(j < 3, 0, jnp.where(j < 6, 1 + 2 * j, jnp.where(j < 7, 1, 2))))
-    return jnp.where(i >= 16, 13 + 2 * (i - 16), jnp.where(lax.rem(i, 2) == 1, odd, even))
+    at = jnp.where(x == 0, 0, 1)
+    even = jnp.where(j < 2, jnp.where(j == at, 0, 3), jnp.where(j < 4, 2 * j + 1, jnp.where(j < 6, j - 3, 2 * j - 3)))
+    return jnp.where(i >= 16, 13 + 2 * (i - 16), jnp.where(lax.rem(i, 2) == 1, 4 + 2 * j, even))
 
 
 def children(t, y, z):
@@ -152,10 +159,12 @@
 
 
 def front_kernel(mat, out, fac, ap_out, top, buf, ap, m0, m1, tmp,
-                 load_sem, pace, x_send, x_recv, t_send, t_recv, p_send, lead_recv, u_recv, out_sem, f_send, f_recv, f_own):
+                 load_sem, pace, c_send, x_send, x_recv, t_send, t_recv, p_send, lead_recv, u_recv, out_sem, f_send, f_recv, f_own):
     core, y, z, x = place()
     root = (y == 0) & (z == 0)
     inner = jnp.logical_not(root)
+    firsts = [depth(t, y, z) == 1 for t in range(4)]
+    child = firsts[0] | firsts[1] | firsts[2] | firsts[3]
     other = 1 - core
 
     def tile_load(s, dst, sem):
@@ -176,22 +185,26 @@
             def _():
                 for cp in tile_load(0, ap.at[c, k], load_sem.at[8]):
                     cp.start()
-    for k in range(2):
-        @pl.when(root & (core == k))
-        def _():
-            for s in range(8):
-                for cp in tile_load(s, buf.at[item_rows(item(k, s))], load_sem.at[s]):
-                    cp.start()
+    def row_loads(tiles):
+        for k in range(2):
+            @pl.when(root & (core == k))
+            def _():
+                for s in tiles:
+                    for cp in tile_load(s, buf.at[item_rows(item(k, s))], load_sem.at[s]):
+                        cp.start()
+
+    row_loads((0,))
 
     barrier = pltpu.get_barrier_semaphore()
     peers = [device(y, z, other, x)]
     for c in range(2):
-        peers += [device(y, z, c, x + 1), device(y, z, c, x + 3)]
+        peers += [device(y, z, c, x + d) for d in (1, 2, 3)]
         for dy, dz in ((1, 0), (3, 0), (0, 1), (0, 3)):
             peers.append(device(y + dy, z + dz, c, x))
     for peer in peers:
         pl.semaphore_signal(barrier, inc=1, device_id=peer, device_id_type=MESH)
     pl.semaphore_wait(barrier, len(peers))
+    row_loads(range(1, 8))
 
     def x_copy(c, k, part, slot, dx):
         rows = pl.ds(Q * part, Q)
@@ -200,6 +213,11 @@
             send_sem=x_send.at[c, k, part, slot], recv_sem=x_recv.at[c, k, part],
             device_id=device(y, z, 0, x + dx), device_id_type=MESH)
 
+    def x_sends(c, k):
+        for part in range(4):
+            x_copy(c, k, part, 0, 1).start()
+            x_copy(c, k, 3 - part, 1, 3).start()
+
     for k in range(2):
         for c in range(2):
             @pl.when((x == k) & (core == c))
@@ -209,11 +227,10 @@
                 if c == 1:
                     for part in range(4):
                         x_copy(c, k, part, 2, 0).start()
-                @pl.when(inner if (c, k) != (0, 0) else core == 0)
-                def _():
-                    for part in range(4):
-                        x_copy(c, k, part, 0, 1).start()
-                        x_copy(c, k, 3 - part, 1, 3).start()
+                away = inner & jnp.logical_not(child)
+                @pl.when(away)
+                def _():
+                    x_sends(c, k)
 
     def x_far(k, part):
         return lax.rem(k + (1 if part < 2 else 3), 4), (1 if part < 2 else 3)
@@ -234,9 +251,7 @@
         def _():
             for part in range(4):
                 x_wait(1, k, part)
-            for part in range(4):
-                x_copy(1, k, part, 0, 1).start()
-                x_copy(1, k, 3 - part, 1, 3).start()
+            x_sends(1, k)
 
     def root_rest(c, k, part):
         fwd, _dx = x_far(k, part)
@@ -274,40 +289,65 @@
     def own_copy(t, n, h):
         return pltpu.make_async_copy(buf.at[piece(t, n, h)], out.at[out_piece(t, n, h)], out_sem.at[n - LEADS])
 
-    for k in range(2):
-        @pl.when(root & (core == k))
-        def _():
-            for n in ORDER:
-                if n < LEADS:
-                    if k == 1:
-                        continue
-                    c, kk = ((0, 0), (1, 0), (1, 1))[n]
-                    src = ap.at[c, kk]
-                    if n == 1:
-                        x_forward(1, 0)
-                        x_forward(1, 1)
-                else:
-                    if (n - LEADS) % 2 != k:
-                        continue
-                    c, src = None, None
-                    s = (n - LEADS) // 2
-                    if k == 1 and s > 0:
-                        pl.semaphore_wait(pace, 1)
-                    for cp in tile_load(s, buf.at[item_rows(n)], load_sem.at[s]):
-                        cp.wait()
+    def root_tree(n, src):
+        for t in range(4):
+            (_, dy, dz), _b, _c = children(t, y, z)
+            for h in range(PIECES):
+                tree_copy(t, n, h, 0, dy, dz, src).start()
+
+    @pl.when(root & (core == 0))
+    def _():
+        @pl.when(x == 0)
+        def _():
+            root_tree(0, ap.at[0, 0])
+        for k in range(2):
+            root_send(k)
+        @pl.when(x == 0)
+        def _():
+            x_sends(0, 0)
+        for n in EVEN:
+            if n < LEADS:
+                kk = n - 1
+                if n == 1:
+                    x_forward(1, 0)
+                    x_forward(1, 1)
                 for t in range(4):
-                    if c is not None:
-                        root_rest(c, kk, t)
-                    (_, dy, dz), _b, _c = children(t, y, z)
-                    for h in range(PIECES):
-                        tree_copy(t, n, h, 0, dy, dz, src).start()
-                if k == 0 and n == 3:
-                    root_send(0)
-                if k == 0 and n == 5:
-                    x_forward(0, 0)
-                    root_send(1)
-                if k == 0 and n in ORDER[:14:2]:
-                    pl.semaphore_signal(pace, inc=1, device_id=device(y, z, other, x), device_id_type=MESH)
+                    root_rest(1, kk, t)
+                root_tree(n, ap.at[1, kk])
+            else:
+                for cp in tile_load((n - LEADS) // 2, buf.at[item_rows(n)], load_sem.at[(n - LEADS) // 2]):
+                    cp.wait()
+                root_tree(n, None)
+            if n == 9:
+                x_forward(0, 0)
+            if n in EVEN[:7]:
+                pl.semaphore_signal(pace, inc=1, device_id=device(y, z, other, x), device_id_type=MESH)
+        for t in range(4):
+            root_rest(0, 0, t)
+
+    @pl.when(root & (core == 1))
+    def _():
+        for n in ODD:
+            for cp in tile_load((n - LEADS) // 2, buf.at[item_rows(n)], load_sem.at[(n - LEADS) // 2]):
+                cp.wait()
+            if n > 4:
+                pl.semaphore_wait(pace, 1)
+            root_tree(n, None)
+
+    def cross_copy(t, h, slot):
+        rows = piece(t, 0, h)
+        return pltpu.make_async_remote_copy(
+            src_ref=buf.at[rows], dst_ref=buf.at[rows],
+            send_sem=c_send.at[slot], recv_sem=t_recv.at[t, h],
+            device_id=device(y, z, 1, x + slot + 1), device_id_type=MESH)
+
+    @pl.when(child & (core == 0) & (x < 2))
+    def _():
+        pl.semaphore_wait(pace, 1)
+        for k in range(2):
+            @pl.when(x == k)
+            def _():
+                x_sends(0, k)
 
     @pl.when(inner & (core == 0))
     def _():
@@ -323,12 +363,16 @@
             i = step - skews[t]
             @pl.when((i >= 0) & (i < PIECES * NITEM))
             def _():
-                n, h = at_step(i // PIECES), lax.rem(i, PIECES)
+                n, h = at_step(i // PIECES, x), lax.rem(i, PIECES)
                 tree_copy(t, n, h, 0, 0, 1).wait_recv()
                 for slot, (cond, dy, dz) in enumerate(children(t, y, z)):
                     @pl.when(cond)
                     def _():
                         tree_copy(t, n, h, slot, dy, dz).start()
+                @pl.when((n == 0) & (x == 0) & firsts[t])
+                def _():
+                    for slot in (0, 2, 1):
+                        cross_copy(t, h, slot).start()
                 @pl.when(n < LEADS)
                 def _():
                     lead_copy(t, n, h).start()
@@ -336,6 +380,14 @@
                 def _():
                     u_copy(t, n, h).start()
                     own_copy(t, n, h).start()
+
+        @pl.when((step == GATE) & child & (x < 2))
+        def _():
+            for k in range(2):
+                @pl.when(x == k)
+                def _():
+                    x_sends(1, k)
+            pl.semaphore_signal(pace, inc=1, device_id=device(y, z, other, x), device_id_type=MESH)
         return 0
 
     @pl.when(inner & (core == 1))
@@ -376,7 +428,9 @@
         src, dst = result(i, 0)
         return pltpu.make_async_copy(src, dst, f_own.at[i])
 
-    @pl.when(core == 0)
+    work = inner | (x < 2)
+
+    @pl.when((core == 0) & work)
     def _():
         eye = jnp.where(
             lax.broadcasted_iota(jnp.int32, (NB, NB), 0) == lax.broadcasted_iota(jnp.int32, (NB, NB), 1), 1.0, 0.0
@@ -438,9 +492,11 @@
             for i in range(16):
                 pltpu.make_async_copy(
                     buf.at[pl.ds((LEADS + i) * NB, NB)], out.at[pl.ds(i * NB, NB)], out_sem.at[i]).wait()
-        for i in range(5):
-            hand(i).wait_recv()
-        @pl.when(root)
+        @pl.when(work)
+        def _():
+            for i in range(5):
+                hand(i).wait_recv()
+        @pl.when(root & work)
         def _():
             hand(5).wait_recv()
 
@@ -476,10 +532,15 @@
                 def _():
                     sent(t_send.at[t, slot], NITEM)
             sent(p_send.at[t], NITEM)
+            @pl.when((x == 0) & firsts[t])
+            def _():
+                for slot in range(3):
+                    sent(c_send.at[slot], 1)
         for k in range(2):
-            @pl.when(root & (core == k))
-            def _():
-                sent(t_send.at[t, 0], 8 + (LEADS if k == 0 else 0))
+            for lead in ((2, 3) if k == 0 else (0,)):
+                @pl.when(root & (core == k) & (jnp.where(x == 0, 3, 2) == lead if k == 0 else core == k))
+                def _():
+                    sent(t_send.at[t, 0], 8 + lead)
 
 
 def front(mat):
@@ -501,7 +562,7 @@
             pltpu.VMEM((2 * NB, NB), F32),
             pltpu.VMEM((2 * NB, NB), F32),
             pltpu.VMEM((NB, NB), F32),
-            dma((9, 4)), pltpu.SemaphoreType.REGULAR, dma((2, 2, 4, 3)), dma((2, 2, 4)), dma((4, 3)), dma((4, NITEM * PIECES)),
+            dma((9, 4)), pltpu.SemaphoreType.REGULAR, dma((3,)), dma((2, 2, 4, 3)), dma((2, 2, 4)), dma((4, 3)), dma((4, NITEM * PIECES)),
             dma((4,)), dma((LEADS,)), dma((16,)), dma((16,)), dma((6,)), dma((6,)), dma((6,)),
         ],
         compiler_params=pltpu.CompilerParams(

time: 120 us -> 111 us (0.925)
  Pallas kernels: 120 us -> 111 us
    pallas_call x1, Pallas kernels: 94.4 us -> 85.1 us  [front(): pl.pallas_call(front_kernel, out_shape=(jax.ShapeDtypeStruct((16 * NB, NB...]
where the time goes in v4:
time: 111 us
  Pallas kernels  111 us (100%)
    pallas_call x1, Pallas kernels, front(): pl.pallas_call(front_kernel, out_shape=(jax.ShapeDtypeStruct((16 * NB, NB...  85.1 us
    pallas_call x1, Pallas kernels, trail(): pl.pallas_call(trail_kernel, out_shape=jax.ShapeDtypeStruct(mat.shape, F3...  25.6 us

profile of v4, /device:TPU:47, one launch (start us, length us, event | category | flops | bytes accessed | tf_op | source)
XLA Modules:
  0.0 110.9 jit_solution(9620564160679819188)
XLA Ops:
  0.0 85.1 %shard_map.17 = (f32[8192,512]{1,0:T(8,128)}, f32[3,512,512]{2,1,0:T(8,128)}, f32[2,512,512]{2,1,0:T(8,128)}, f32[512,512]{1,0:T(8,128)}) custom-call(f32[512,32,1,128]{3,2,1,0:T(1,128)} %bitcast.2), custom_call_target="tpu_custom_call" | custom-call | tf_op jit(solution)/shard_map/pallas_call | solution.py:549
  85.1 25.6 %shard_map.18 = f32[512,32,1,128]{3,2,1,0:T(1,128)} custom-call(f32[512,32,1,128]{3,2,1,0:T(1,128)} %bitcast.3, f32[8192,512]{1,0:T(8,128)} %get-tuple-element.9.u, f32[3,512,512]{2,1,0:T(8,128)} %get-tuple-element.10.fac, f32[2,512,512]{2,1,0:T(8,128)} %get-tuple-element.11.ap, f32[512,512]{1,0:T(8,128)} %get-tuple-element.12.top), custom_call_target="tpu_custom_call" | custom-call | tf_op jit(solution)/shard_map/pallas_call | solution.py:665

commit v5 on v4

--- a/solution.py
+++ b/solution.py
@@ -304,7 +304,8 @@
             root_send(k)
         @pl.when(x == 0)
         def _():
-            x_sends(0, 0)
+            for part in range(4):
+                x_copy(0, 0, part, 0, 1).start()
         for n in EVEN:
             if n < LEADS:
                 kk = n - 1
@@ -318,12 +319,12 @@
                 for cp in tile_load((n - LEADS) // 2, buf.at[item_rows(n)], load_sem.at[(n - LEADS) // 2]):
                     cp.wait()
                 root_tree(n, None)
-            if n == 9:
-                x_forward(0, 0)
             if n in EVEN[:7]:
                 pl.semaphore_signal(pace, inc=1, device_id=device(y, z, other, x), device_id_type=MESH)
-        for t in range(4):
-            root_rest(0, 0, t)
+        @pl.when(x == 1)
+        def _():
+            for part in range(4):
+                x_wait(0, 0, part)
 
     @pl.when(root & (core == 1))
     def _():
@@ -508,13 +509,15 @@
                 @pl.when((x == k) & sender)
                 def _():
                     x_copy(c, k, part, 0, 1).wait_send()
-                    x_copy(c, k, part, 1, 3).wait_send()
+                    @pl.when(inner if (c, k) == (0, 0) else x == k)
+                    def _():
+                        x_copy(c, k, part, 1, 3).wait_send()
                 if c == 1:
                     @pl.when((x == k) & (core == 1))
                     def _():
                         x_copy(c, k, part, 2, 0).wait_send()
                 passed = (x == fwd) & (core == 0)
-                @pl.when(passed & inner if (c, k) == (0, 1) else passed)
+                @pl.when(passed & inner if c == 0 else passed)
                 def _():
                     x_copy(c, k, part, 0, 1).wait_send()
 
@@ -611,10 +614,11 @@
     ]
     for cp in first:
         cp.start()
-    for s in range(8):
-        u_copy(s).start()
-        for cp in s_copies(s):
-            cp.start()
+    def load(tiles):
+        for s in tiles:
+            u_copy(s).start()
+            for cp in s_copies(s):
+                cp.start()
 
     first[0].wait()
     first[1].wait()
@@ -625,14 +629,15 @@
     l10 = split(fv[1])
     rest = av[1] - dot3(split(x0), l10, NT)
     first[4].wait()
+    load(range(8))
     inv1 = split(fv[2])
     x1 = tri(split(rest), inv1)
     v = tri_t(split(x1), inv1)
     vs = split(v)
     ws = split(tri_t(split(x0 - dot3(vs, l10, NN)), inv0))
-    for i in range(2):
-        whl[i, :, :NB] = ws[i]
-        whl[i, :, NB:] = vs[i]
+    for i, h in enumerate((0, 0, 1)):
+        whl[:, 2 * NB * i:2 * NB * i + NB] = ws[h]
+        whl[:, 2 * NB * i + NB:2 * NB * (i + 1)] = vs[h]
     first[5].wait()
     own = jnp.where((p == 0) & (x > 0), 0.0, tv[...])
     av[0] = jnp.where(p < 2, own, jnp.where(x == 0, x0, x1))
@@ -646,8 +651,9 @@
             cp.wait()
         for h in range(2):
             cols = pl.ds(256 * h, 256)
-            part = split(ubuf[s, :, cols])
-            new = sbuf[s, :, cols] - dot3((whl[0], whl[1]), part, NN)
+            uh, ul = split(ubuf[s, :, cols])
+            part = jnp.concatenate([uh, ul, uh], 0)
+            new = sbuf[s, :, cols] - lax.dot_general(whl[...], part, NN, preferred_element_type=F32)
             new = jnp.where(p < 2, 0.0, new)
             if s == 0:
                 new = jnp.where(x < 2, av[0, :, cols], new)
@@ -669,7 +675,7 @@
         out_specs=hb,
         scratch_shapes=[
             pltpu.VMEM((3, NB, NB), F32), pltpu.VMEM((2, NB, NB), F32), pltpu.VMEM((NB, NB), F32),
-            pltpu.VMEM((2, NB, 2 * NB), BF),
+            pltpu.VMEM((NB, 6 * NB), BF),
             pltpu.VMEM((8, NB, NB), F32), pltpu.VMEM((8, 2 * NB, NB), F32), pltpu.VMEM((3, NB, NB), F32),
             dma((6,)), dma((8, 4)), dma((8,)), dma((3, 4)),
         ],

time: 111 us -> 109 us (0.982)
  Pallas kernels: 111 us -> 109 us
    pallas_call x1, Pallas kernels: 85.1 us -> 83.4 us  [front(): pl.pallas_call(front_kernel, out_shape=(jax.ShapeDtypeStruct((16 * NB, NB...]
where the time goes in v5:
time: 109 us
  Pallas kernels  109 us (100%)
    pallas_call x1, Pallas kernels, front(): pl.pallas_call(front_kernel, out_shape=(jax.ShapeDtypeStruct((16 * NB, NB...  83.4 us
    pallas_call x1, Pallas kernels, trail(): pl.pallas_call(trail_kernel, out_shape=jax.ShapeDtypeStruct(mat.shape, F3...  25.6 us

profile of v5, /device:TPU:47, one launch (start us, length us, event | category | flops | bytes accessed | tf_op | source)
XLA Modules:
  0.0 109.2 jit_solution(1681962359065060544)
XLA Ops:
  0.0 83.4 %shard_map.17 = (f32[8192,512]{1,0:T(8,128)}, f32[3,512,512]{2,1,0:T(8,128)}, f32[2,512,512]{2,1,0:T(8,128)}, f32[512,512]{1,0:T(8,128)}) custom-call(f32[512,32,1,128]{3,2,1,0:T(1,128)} %bitcast.2), custom_call_target="tpu_custom_call" | custom-call | tf_op jit(solution)/shard_map/pallas_call | solution.py:552
  83.4 25.6 %shard_map.18 = f32[512,32,1,128]{3,2,1,0:T(1,128)} custom-call(f32[512,32,1,128]{3,2,1,0:T(1,128)} %bitcast.3, f32[8192,512]{1,0:T(8,128)} %get-tuple-element.9.u, f32[3,512,512]{2,1,0:T(8,128)} %get-tuple-element.10.fac, f32[2,512,512]{2,1,0:T(8,128)} %get-tuple-element.11.ap, f32[512,512]{1,0:T(8,128)} %get-tuple-element.12.top), custom_call_target="tpu_custom_call" | custom-call | tf_op jit(solution)/shard_map/pallas_call | solution.py:671
